TPU v7x, 32 devices: a 4x4x1 block of a 4x4x8 slice. The times are simulated.
32 devices in a mesh: dp: 1 (over z), col: 4 (over y), row: 8 (over x, core).
Axes of the slice: x: 4, y: 4, z: 1, core: 2. Of those that a mesh axis runs over, the one named last changes fastest.
The devices are a block of a 4x4x8 slice.
Arguments:
- x_act: bfloat16 [2048, 8192], P(('dp', 'row'), 'col')
- ln_gain: float32 [8192], P('col')
- w_in: bfloat16 [8192, 28672], P('row', 'col')
- w_out: bfloat16 [28672, 8192], P('row', 'col')
Outputs:
- output: bfloat16 [2048, 8192], P(('dp', 'row'), 'col')
All inputs are finite; a program needn't handle non-finite values.
Results may differ from a plain program's by a relative error of at most 0.00133.
Values are sent between devices in bfloat16 or wider.
A program may use at most 768 MiB of HBM per device.

v0:
```python
import jax
import jax.numpy as jnp
from jax import lax
from jax.sharding import PartitionSpec as P

NORM_EPS = 1e-5


def solution(mesh):
    col_size = mesh.shape["col"]

    def local_block(x_blk, gain_blk, w_in_blk, w_out_blk):
        d_model = x_blk.shape[1] * col_size
        x_f32 = x_blk.astype(jnp.float32)
        part_stats = jnp.stack([jnp.sum(x_f32, axis=1), jnp.sum(x_f32 * x_f32, axis=1)])
        row_stats = lax.psum(part_stats, "col") / d_model
        row_mean = row_stats[0][:, None]
        row_var = row_stats[1][:, None] - row_mean * row_mean
        z_blk = ((x_f32 - row_mean) * lax.rsqrt(row_var + NORM_EPS) * gain_blk).astype(jnp.bfloat16)
        z_rows = lax.all_gather(z_blk, "col", axis=1, tiled=True)
        z_cols = lax.all_to_all(z_rows, "row", 1, 0, tiled=True)
        up_part = jnp.dot(z_cols, w_in_blk, preferred_element_type=jnp.float32)
        up_sum = lax.psum_scatter(up_part, "row", scatter_dimension=0, tiled=True)
        h_blk = jax.nn.gelu(up_sum, approximate=True).astype(jnp.bfloat16)
        h_rows = lax.all_gather(h_blk, "col", axis=1, tiled=True)
        h_cols = lax.all_to_all(h_rows, "row", 1, 0, tiled=True)
        down_part = jnp.dot(h_cols, w_out_blk, preferred_element_type=jnp.float32)
        down_sum = lax.psum_scatter(down_part, "row", scatter_dimension=0, tiled=True)
        return (x_f32 + down_sum).astype(jnp.bfloat16)

    return jax.shard_map(
        local_block,
        mesh=mesh,
        in_specs=(P(("dp", "row"), "col"), P("col"), P("row", "col"), P("row", "col")),
        out_specs=P(("dp", "row"), "col"),
        check_vma=False,
    )
```

profile of v0, /device:TPU:96, one launch (start us, length us, event | category | flops | bytes accessed | tf_op | source)
XLA Modules:
  0.0 897.9 jit_solution(16837343801383913133)
XLA Ops:
  6.5 0.0 all-gather.3.cloned.1.call-start
  6.6 1.7 convert_reduce_fusion
  8.3 11.8 %psum.7 = f32[2,256]{1,0:T(2,128)S(1)} all-reduce(f32[2,256]{1,0:T(2,128)S(1)} %pad_maximum_fusion), channel_id=1, replica_groups=mesh['dp'=1,'col'=4,'row'=8] {'col'}, use_global_device_ids=true, to_apply=%region_2.0 | all-reduce | flops 512 | bytes 4096 | tf_op jit(solution)/shard_map/psum | solution.py:16
  20.1 2.6 fusion.11
  22.7 0.1 all-gather.3.cloned.1.call-update
  22.8 0.1 reduce-scatter.3.cloned.1.call-start
  22.8 45.0 %all-gather.3.cloned.1.call-done = bf16[256,8192]{1,0:T(8,128)(2,1)} async-done(((bf16[256,2048]{1,0:T(8,128)(2,1)}), bf16[256,8192]{1,0:T(8,128)(2,1)}) %all-gather.3.cloned.1.call-update) | async-done | bytes 4194320 | tf_op jit(solution)/shard_map/all_gather | solution.py:20
  67.8 2.6 copy.12
  70.5 53.8 %all_to_all.38 = bf16[256,8,1024]{2,0,1:T(8,128)(2,1)S(1)} all-to-all(bf16[256,8,1024]{2,0,1:T(8,128)(2,1)S(1)} %bitcast.23), channel_id=1, replica_groups=mesh['dp'=1,'col'=4,'row'=8] {'row'}, dimensions={1} | all-to-all | bytes 8388608 | tf_op jit(solution)/shard_map/all_to_all | solution.py:21
  124.3 38.8 %fusion.14 = f32[2048,7168]{1,0:T(8,128)} fusion(bf16[2048,1024]{1,0:T(8,128)(2,1)S(1)} %bitcast.27, bf16[1024,7168]{1,0:T(8,128)(2,1)} %param.6), kind=kOutput, calls=%fused_computation.24 | convolution fusion | flops 30064771072 | bytes 77594624 | tf_op jit(solution)/shard_map/dot_general | solution.py:22
  163.1 0.1 reduce-scatter.3.cloned.1.call-update
  163.1 0.1 all-gather.5.cloned.1.call-start
  163.2 284.9 %reduce-scatter.3.cloned.1.call-done = f32[256,7168]{1,0:T(8,128)} async-done(((f32[2048,7168]{1,0:T(8,128)}), f32[256,7168]{1,0:T(8,128)}) %reduce-scatter.3.cloned.1.call-update) | async-done | bytes 7340048 | tf_op jit(solution)/shard_map/reduce_scatter | solution.py:23
  448.1 5.6 fusion.7
  453.7 0.1 all-gather.5.cloned.1.call-update
  453.8 0.1 reduce-scatter.5.cloned.1.call-start
  453.8 134.2 %all-gather.5.cloned.1.call-done = bf16[256,28672]{1,0:T(8,128)(2,1)} async-done(((bf16[256,7168]{1,0:T(8,128)(2,1)}), bf16[256,28672]{1,0:T(8,128)(2,1)}) %all-gather.5.cloned.1.call-update) | async-done | bytes 14680080 | tf_op jit(solution)/shard_map/all_gather | solution.py:25
  588.1 7.5 copy.11
  595.6 166.2 %all_to_all.39 = bf16[256,8,3584]{2,0,1:T(8,128)(2,1)} all-to-all(bf16[256,8,3584]{2,0,1:T(8,128)(2,1)S(1)} %bitcast.22), channel_id=1, replica_groups=mesh['dp'=1,'col'=4,'row'=8] {'row'}, dimensions={1} | all-to-all | bytes 29360128 | tf_op jit(solution)/shard_map/all_to_all | solution.py:26
  761.8 38.2 %fusion.15 = f32[2048,2048]{1,0:T(8,128)} fusion(bf16[2048,3584]{1,0:T(8,128)(2,1)} %bitcast.25, bf16[3584,2048]{1,0:T(8,128)(2,1)} %param.7), kind=kOutput, calls=%fused_computation.25 | convolution fusion | flops 30064771072 | bytes 46137344 | tf_op jit(solution)/shard_map/dot_general | solution.py:27
  799.9 0.0 copy-start
  799.9 0.1 reduce-scatter.5.cloned.1.call-update
  800.0 88.5 %reduce-scatter.5.cloned.1.call-done = f32[256,2048]{1,0:T(8,128)} async-done(((f32[2048,2048]{1,0:T(8,128)}), f32[256,2048]{1,0:T(8,128)}) %reduce-scatter.5.cloned.1.call-update) | async-done | bytes 2097168 | tf_op jit(solution)/shard_map/reduce_scatter | solution.py:28
  888.5 0.0 copy-done
  888.5 2.8 fusion.12
  (4 shorter events, 0.0 us)
Async XLA Ops:
  6.5 61.3 %all-gather.3.cloned.1.call-start = ((), (), s32[]{:S(2)}) async-start(), calls=%async_computation.4 | async-start | bytes 5242880 | tf_op jit(solution)/shard_map/all_gather | solution.py:20
  22.8 425.4 %reduce-scatter.3.cloned.1.call-start = ((), (), s32[]{:S(2)}) async-start(), calls=%async_computation.5 | async-start | bytes 66060288 | tf_op jit(solution)/shard_map/reduce_scatter | solution.py:23
  163.1 424.9 %all-gather.5.cloned.1.call-start = ((), (), s32[]{:S(2)}) async-start(), calls=%async_computation.6 | async-start | bytes 18350080 | tf_op jit(solution)/shard_map/all_gather | solution.py:25
  453.8 434.8 %reduce-scatter.5.cloned.1.call-start = ((), (), s32[]{:S(2)}) async-start(), calls=%async_computation.7 | async-start | bytes 18874368 | tf_op jit(solution)/shard_map/reduce_scatter | solution.py:28
  799.9 88.6 %copy-start = (bf16[256,2048]{1,0:T(8,128)(2,1)S(1)}, bf16[256,2048]{1,0:T(8,128)(2,1)}, u32[]{:S(2)}) copy-start(bf16[256,2048]{1,0:T(8,128)(2,1)} %param.4) | copy-start | bytes 3145732
Sparse Core Ops, SparseCore 0:
  22.9 44.9 all-gather.2
  163.3 284.8 reduce-scatter.2
  453.9 134.1 all-gather.4
  800.1 88.3 reduce-scatter.4
where the time goes:
time: 899 us; the launch traced here: 898 us
  waiting for transfers between devices  553 us (62%)
  blocking collectives  232 us (26%)
  matrix products  76.9 us (9%)
  between operations  13.2 us (1%)
  other arithmetic  12.7 us (1%)
  local copies, waits for them, and re-layouts  10.2 us (1%)
    reduce_scatter x1, waiting for transfers between devices, local_block(): up_sum = lax.psum_scatter(up_part, 'row', scatter_dimension=0, tiled=True)  285 us
    all_to_all x1, blocking collectives, local_block(): h_cols = lax.all_to_all(h_rows, 'row', 1, 0, tiled=True)  166 us
    all_gather x1, waiting for transfers between devices, local_block(): h_rows = lax.all_gather(h_blk, 'col', axis=1, tiled=True)  134 us
    reduce_scatter x1, waiting for transfers between devices, local_block(): lax.psum_scatter(down_part, 'row', scatter_dimension=0, tiled=True)  88.5 us
    all_to_all x1, blocking collectives, local_block(): z_cols = lax.all_to_all(z_rows, 'row', 1, 0, tiled=True)  53.8 us
    all_gather x1, waiting for transfers between devices, local_block(): z_rows = lax.all_gather(z_blk, 'col', axis=1, tiled=True)  45 us
    dot_general x1, matrix products, local_block(): up_part = jnp.dot(z_cols, w_in_blk, preferred_element_type=jnp.float32)  38.8 us
    dot_general x1, matrix products, local_block(): down_part = jnp.dot(h_cols, w_out_blk, preferred_element_type=jnp.float32)  38.2 us
  transfers between devices with their start and end apart: 4, of which 4 were waited for; matrix products, arithmetic and copies ran while one was open for 0% of the time, Pallas kernels for 0%

commit v1 on v0

v1 whole, which is shorter than its diff:
```python
import functools

import jax
import jax.numpy as jnp
from jax import lax
from jax.experimental import pallas as pl
from jax.experimental.pallas import tpu as pltpu
from jax.sharding import PartitionSpec as P

NORM_EPS = 1e-5
MESH = pl.DeviceIdType.MESH
SUB = 4
LATE = 3


def gelu(v):
    return 0.5 * v * (1.0 + jnp.tanh(0.7978845608028654 * (v + 0.044715 * (v * v * v))))


class Sems:
    def __init__(self):
        self.base, self.total = {}, 0

    def add(self, name, count):
        self.base[name] = self.total
        self.total += count

    def __call__(self, name, index=0):
        return self.base[name] + index


def plan(tiles):
    s = Sems()
    for name, count in (
        ("stat", 3), ("zx", 4), ("zy", 16), ("w", 3 * tiles), ("wo", tiles), ("wf", 3 * tiles),
        ("wout", 1), ("h1a", 3), ("h1b", 3 * SUB), ("h2", 6 * SUB), ("ag", 8 * SUB), ("y", 3 * SUB),
    ):
        s.add(name, count)
    return s


def block(n, x_hbm, gain_ref, win, wout, y_hbm, w_hbm, wo_hbm, hst_a, hst_b, yr_hbm,
          xv, stat, z, wt, hm_a, hm_b, hf_a, hf_b, acc, wot, yt, ov, ss, rs, ls):
    nx, ny, d_model = n
    row, cy = lax.axis_index("row"), lax.axis_index("col")
    cx, k = row // 2, lax.rem(row, 2)
    tok, dloc = xv.shape
    tiles, krows, tw = w_hbm.shape[0], w_hbm.shape[2], w_hbm.shape[3]
    early = tiles - LATE
    half = tok // 2
    sub = tok // SUB
    sem = plan(tiles)

    def ring(v, d, m):
        return lax.rem(v + (d + m), m)

    def dev(dx=0, dy=0, core=None):
        return {"row": 2 * ring(cx, dx, nx) + (k if core is None else core), "col": ring(cy, dy, ny)}

    partner = dev(core=1 - k)

    def remote(src, dst, where, i):
        return pltpu.make_async_remote_copy(
            src_ref=src, dst_ref=dst, send_sem=ss.at[i], recv_sem=rs.at[i], device_id=where, device_id_type=MESH
        )

    sends, z_sends = [], []

    def send(src, dst, where, i, log=sends):
        c = remote(src, dst, where, i)
        c.start()
        log.append(c)

    def got(ref, i):
        remote(ref, ref, partner, i).wait_recv()

    load_x = pltpu.make_async_copy(x_hbm, xv, ls.at[0])
    load_x.start()
    barrier = pltpu.get_barrier_semaphore()
    peers = [partner] + [dev(dx=d) for d in range(1, nx)] + [dev(dy=d) for d in range(1, ny)]
    for p in peers:
        pl.semaphore_signal(barrier, inc=1, device_id=p, device_id_type=MESH)
    load_x.wait()

    lane = lax.broadcasted_iota(jnp.int32, stat.shape[1:], 1)

    def part(i, _):
        at = pl.ds(pl.multiple_of(i * 32, 32), 32)
        v = xv[at, :].astype(jnp.float32)
        s1 = jnp.sum(v, axis=1, keepdims=True)
        s2 = jnp.sum(v * v, axis=1, keepdims=True)
        stat[0, at, :] = jnp.where(lane[:32] == 0, s1, s2)
        return 0

    lax.fori_loop(0, tok // 32, part, 0)
    pl.semaphore_wait(barrier, len(peers))
    for d in range(1, ny):
        send(stat.at[0], stat.at[d], dev(dy=d), sem("stat", d - 1))

    def columns(dx, t):
        return pl.ds(pl.multiple_of(ring(cx, dx, nx) * (tiles * tw) + t * tw, 128), tw)

    def w_issue(t):
        for d in (1, 3, 2):
            send(win.at[:, columns(d, t)], w_hbm.at[t, row], dev(dx=d), sem("w", 3 * t + d - 1))
        send(win.at[:, columns(0, t)], w_hbm.at[t, row], partner, sem("wo", t))

    def w_forward(t):
        for d in (1, 3, 2):
            slot = 2 * ring(cx, -d, nx) + k
            got(w_hbm.at[t, slot], sem("w", 3 * t + d - 1))
            send(w_hbm.at[t, slot], w_hbm.at[t, slot], partner, sem("wf", 3 * t + d - 1))

    def w_ready(t):
        got(w_hbm.at[t, row], sem("wo", t))
        for d in (1, 3, 2):
            got(w_hbm.at[t, row], sem("wf", 3 * t + d - 1))

    w_issue(0)
    send(wout, wo_hbm, partner, sem("wout"))

    for d in range(1, ny):
        got(stat.at[d], sem("stat", d - 1))

    def norm(i, _):
        at = pl.ds(pl.multiple_of(i * 32, 32), 32)
        total = (stat[0, at, :] + stat[1, at, :]) + (stat[2, at, :] + stat[3, at, :])
        mean = total[:, 0:1] / d_model
        var = total[:, 1:2] / d_model - mean * mean
        v = xv[at, :].astype(jnp.float32)
        z[cx, cy, at, :] = ((v - mean) * lax.rsqrt(var + NORM_EPS) * gain_ref[...]).astype(z.dtype)
        return 0

    lax.fori_loop(0, tok // 32, norm, 0)

    off = (0, 1, 3, 2)
    lo, hi = pl.ds(0, half), pl.ds(half, half)

    def zb(b, dy, rows=None):
        ref = z.at[ring(cx, off[b], nx), ring(cy, dy, ny)]
        return ref if rows is None else ref.at[rows]

    def zx_send():
        send(zb(0, 0), zb(0, 0), dev(dx=1), sem("zx", 0), z_sends)
        send(zb(0, 0), zb(0, 0), dev(dx=-1), sem("zx", 1), z_sends)

    def zx_forward():
        got(zb(2, 0), sem("zx", 0))
        send(zb(2, 0, lo), zb(2, 0, lo), dev(dx=1), sem("zx", 2), z_sends)
        got(zb(1, 0), sem("zx", 1))
        send(zb(1, 0, hi), zb(1, 0, hi), dev(dx=-1), sem("zx", 3), z_sends)

    def zx_last():
        got(zb(3, 0, lo), sem("zx", 2))
        got(zb(3, 0, hi), sem("zx", 3))

    def zy_send(b):
        send(zb(b, 0), zb(b, 0), dev(dy=1), sem("zy", 4 * b), z_sends)
        send(zb(b, 0), zb(b, 0), dev(dy=-1), sem("zy", 4 * b + 1), z_sends)

    def zy_forward(b):
        got(zb(b, -1), sem("zy", 4 * b))
        send(zb(b, -1, lo), zb(b, -1, lo), dev(dy=1), sem("zy", 4 * b + 2), z_sends)
        got(zb(b, 1), sem("zy", 4 * b + 1))
        send(zb(b, 1, hi), zb(b, 1, hi), dev(dy=-1), sem("zy", 4 * b + 3), z_sends)

    def zy_last(b):
        got(zb(b, 2, lo), sem("zy", 4 * b + 2))
        got(zb(b, 2, hi), sem("zy", 4 * b + 3))

    def wt_load(t, slot):
        for j in range(2 * nx):
            r = ring(row, j, 2 * nx)
            dst = wt.at[slot, r // 2, pl.ds(pl.multiple_of(lax.rem(r, 2) * krows, krows), krows)]
            src = win.at[:, columns(0, t)] if j == 0 else w_hbm.at[t, r]
            pltpu.make_async_copy(src, dst, ls.at[1 + slot]).start()

    def wt_wait(slot):
        pltpu.make_async_copy(wt.at[slot], wt.at[slot], ls.at[1 + slot]).wait()

    def up(hm, hf, first, t0, t1, b0, b1):
        wt_load(t0, 0)

        def tile(i, _):
            slot = lax.rem(i, 2)
            wt_wait(slot)

            @pl.when(i + 1 < t1 - t0)
            def _():
                wt_load(t0 + i + 1, 1 - slot)

            at = pl.ds(pl.multiple_of((t0 + i - first) * tw, 128), tw)

            def rows(b, _):
                t = ring(cx, b + b // 2 - 2 * (b // 3), nx)
                v = jnp.dot(z[t, 0], wt[slot, 0], preferred_element_type=jnp.float32)
                for j in range(1, ny):
                    v += jnp.dot(z[t, j], wt[slot, j], preferred_element_type=jnp.float32)
                h = gelu(v).astype(hm.dtype).reshape(SUB, sub, tw)
                hm[t, :, :, at] = h

                @pl.when((t == cy) & (cx == cy))
                def _():
                    hf[cx, :, cy, :, at] = h

                return 0

            lax.fori_loop(b0, b1, rows, 0)
            return 0

        lax.fori_loop(0, t1 - t0, tile, 0)

    def h1_a():
        for d in range(1, ny):
            t = ring(cy, d, ny)
            i = sem("h1a", d - 1)

            @pl.when(cx == cy)
            def _():
                remote(hm_a.at[t], hf_a.at[cx, :, t], dev(dy=d), i).start()

            @pl.when(cx != cy)
            def _():
                remote(hm_a.at[t], hst_a.at[cy], dev(dy=d), i).start()

            sends.append(remote(hm_a.at[t], hst_a.at[cy], dev(dy=d), i))

    def h1_b(s):
        for d in range(1, ny):
            t = ring(cy, d, ny)
            i = sem("h1b", 3 * s + d - 1)

            @pl.when(cx == cy)
            def _():
                remote(hm_b.at[t, s], hf_b.at[cx, s, t], dev(dy=d), i).start()

            @pl.when(cx != cy)
            def _():
                remote(hm_b.at[t, s], hst_b.at[cy, s], dev(dy=d), i).start()

            sends.append(remote(hm_b.at[t, s], hst_b.at[cy, s], dev(dy=d), i))

    def h1_wait(ref, first):
        for d in range(1, ny):
            got(ref, first + d - 1)

    def h2(late, s):
        hm, hst, hf = (hm_b, hst_b, hf_b) if late else (hm_a, hst_a, hf_a)
        for d in (1, 3, 2):
            c = ring(cx, d, nx)
            i = sem("h2", 3 * (late * SUB + s) + d - 1)

            @pl.when(c == cy)
            def _():
                remote(hm.at[cy, s], hf.at[cx, s, cy], dev(dx=d), i).start()

            @pl.when(c != cy)
            def _():
                remote(hst.at[c, s], hf.at[cx, s, cy], dev(dx=d), i).start()

            sends.append(remote(hst.at[c, s], hf.at[cx, s, cy], dev(dx=d), i))

    def ag(late, s):
        hf = hf_b if late else hf_a
        u = late * SUB + s
        for d in (1, 3, 2):
            got(hf.at[ring(cx, -d, nx), s, cy], sem("h2", 3 * u + d - 1))
        mine = hf.at[:, s, cy]
        send(mine, mine, dev(dy=1), sem("ag", 4 * u))
        send(mine, mine, dev(dy=-1), sem("ag", 4 * u + 1))

    def ag_forward(late, s):
        hf = hf_b if late else hf_a
        u = late * SUB + s
        left, right = ring(cy, -1, ny), ring(cy, 1, ny)
        first, second = pl.ds(0, nx // 2), pl.ds(nx // 2, nx // 2)
        got(hf.at[:, s, left], sem("ag", 4 * u))
        send(hf.at[first, s, left], hf.at[first, s, left], dev(dy=1), sem("ag", 4 * u + 2))
        got(hf.at[:, s, right], sem("ag", 4 * u + 1))
        send(hf.at[second, s, right], hf.at[second, s, right], dev(dy=-1), sem("ag", 4 * u + 3))

    def ag_last(late, s):
        hf = hf_b if late else hf_a
        u = late * SUB + s
        far = ring(cy, 2, ny)
        got(hf.at[pl.ds(0, nx // 2), s, far], sem("ag", 4 * u + 2))
        got(hf.at[pl.ds(nx // 2, nx // 2), s, far], sem("ag", 4 * u + 3))

    ew, lw = early * tw, LATE * tw
    depth = wot.shape[1]
    per = ew // depth

    def wot_load(i, slot):
        u, j = i // per, lax.rem(i, per)
        c = 2 * lax.rem(k + u // 2, 2) + lax.rem(u, 2)
        at = pl.ds(pl.multiple_of(lax.rem(u, 2) * (ew + lw) + j * depth, 128), depth)

        @pl.when(u < nx // 2)
        def _():
            pltpu.make_async_copy(wout.at[at], wot.at[slot], ls.at[3 + slot]).start()

        @pl.when(u >= nx // 2)
        def _():
            pltpu.make_async_copy(wo_hbm.at[at], wot.at[slot], ls.at[3 + slot]).start()

        return c, j

    def down_early():
        wot_load(0, 0)

        def step(i, _):
            slot = lax.rem(i, 2)
            pltpu.make_async_copy(wot.at[slot], wot.at[slot], ls.at[3 + slot]).wait()

            @pl.when(i + 1 < nx * per)
            def _():
                wot_load(i + 1, 1 - slot)

            u, j = i // per, lax.rem(i, per)
            c = 2 * lax.rem(k + u // 2, 2) + lax.rem(u, 2)
            at = pl.ds(pl.multiple_of(j * depth, 128), depth)

            def rows(s, _):
                h = hf_a[c, s, :, :, at].reshape(tok, depth)
                v = jnp.dot(h, wot[slot], preferred_element_type=jnp.float32).reshape(acc.shape[1:])

                @pl.when(i == 0)
                def _():
                    acc[s] = v

                @pl.when(i > 0)
                def _():
                    acc[s] += v

                return 0

            lax.fori_loop(0, SUB, rows, 0)
            return 0

        lax.fori_loop(0, nx * per, step, 0)

    def late_weights():
        n3 = lw // tok
        for c in z_sends:
            c.wait_send()

        def fetch(i, _):
            u, j = i // n3, lax.rem(i, n3)
            c = 2 * lax.rem(k + u // 2, 2) + lax.rem(u, 2)
            at = pl.ds(pl.multiple_of(lax.rem(u, 2) * (ew + lw) + ew + j * tok, 128), tok)

            @pl.when(u < nx // 2)
            def _():
                pltpu.make_async_copy(wout.at[at], z.at[c, j], ls.at[5]).start()

            @pl.when(u >= nx // 2)
            def _():
                pltpu.make_async_copy(wo_hbm.at[at], z.at[c, j], ls.at[5]).start()

            return 0

        lax.fori_loop(0, nx * n3, fetch, 0)
        ref = z.at[:, pl.ds(0, n3)]
        pltpu.make_async_copy(ref, ref, ls.at[5]).wait()

    def down_late(s):
        n3 = lw // tok

        def step(c, _):
            h = hf_b[c, s].reshape(tok, lw)
            w = z[c, pl.ds(0, n3)].reshape(lw, dloc)
            acc[s] += jnp.dot(h, w, preferred_element_type=jnp.float32).reshape(acc.shape[1:])
            return 0

        lax.fori_loop(0, nx, step, 0)

    def y_send(s):
        for d in (2, 1, 3):
            send(acc.at[s, ring(cx, d, nx)], yr_hbm.at[d - 1, s], dev(dx=d), sem("y", 3 * s + d - 1))

    def y_final(s):
        for d in range(1, nx):
            got(yr_hbm.at[d - 1, s], sem("y", 3 * s + d - 1))
        c = pltpu.make_async_copy(yr_hbm.at[:, s], yt, ls.at[6])
        c.start()
        c.wait()
        at = pl.ds(s * sub, sub)
        total = (acc[s, cx] + yt[0]) + (yt[1] + yt[2])
        ov[at, :] = (xv[at, :].astype(jnp.float32) + total).astype(ov.dtype)

    zy_send(0)
    zx_send()
    w_issue(1)
    zy_forward(0)
    zx_forward()
    zy_send(1)
    zy_send(2)
    w_forward(0)
    w_issue(2)
    zy_last(0)
    zx_last()
    zy_send(3)
    zy_forward(1)
    zy_forward(2)
    w_forward(1)
    w_issue(3)
    zy_last(1)
    zy_last(2)
    w_forward(2)
    w_issue(4)
    zy_forward(3)
    w_ready(0)
    w_ready(1)
    w_ready(2)
    up(hm_a, hf_a, 0, 0, 3, 0, 3)
    w_forward(3)
    w_issue(5)
    w_ready(3)
    up(hm_a, hf_a, 0, 3, 4, 0, 3)
    zy_last(3)
    up(hm_a, hf_a, 0, 0, 4, 3, 4)
    h1_a()
    w_forward(4)
    w_issue(6)
    h1_wait(hst_a.at[0], sem("h1a"))
    for s in range(SUB):
        h2(0, s)
    w_ready(4)
    up(hm_b, hf_b, early, 4, 5, 0, 4)
    for s in range(SUB):
        ag(0, s)
    w_forward(5)
    w_ready(5)
    up(hm_b, hf_b, early, 5, 6, 0, 4)
    w_forward(6)
    for s in range(SUB):
        ag_forward(0, s)
    w_ready(6)
    up(hm_b, hf_b, early, 6, 7, 0, 4)
    for s in range(SUB):
        h1_b(s)
    for s in range(SUB):
        ag_last(0, s)
    got(wo_hbm, sem("wout"))
    down_early()
    late_weights()
    for s in range(SUB):
        h1_wait(hst_b.at[0, 0], sem("h1b", 3 * s))
        h2(1, s)
    for s in range(SUB):
        ag(1, s)
    for s in range(SUB):
        ag_forward(1, s)
    for s in range(SUB):
        ag_last(1, s)
        down_late(s)
        y_send(s)
        if s > 0:
            y_final(s - 1)
    y_final(SUB - 1)
    out = pltpu.make_async_copy(ov, y_hbm, ls.at[0])
    out.start()
    for c in sends:
        c.wait_send()
    out.wait()


def solution(mesh):
    nx, ny = mesh.shape["row"] // 2, mesh.shape["col"]

    def local_block(x, gain, win, wout):
        tok, dloc = x.shape
        krows, floc = win.shape
        width = floc // nx
        tw = width // 7
        tiles = width // tw
        early = tiles - LATE
        ew, lw = early * tw, LATE * tw
        sub = tok // SUB
        bf, f32 = jnp.bfloat16, jnp.float32
        count = plan(tiles).total
        hbm = lambda shape, dt: jax.ShapeDtypeStruct(shape, dt)
        outs = pl.pallas_call(
            functools.partial(block, (nx, ny, dloc * ny)),
            name="mlp_block",
            out_shape=[
                hbm((tok, dloc), bf),
                hbm((tiles, 2 * nx, krows, tw), bf),
                hbm(wout.shape, bf),
                hbm((ny, SUB, sub, ew), bf),
                hbm((ny, SUB, sub, lw), bf),
                hbm((nx - 1, SUB, sub, dloc), f32),
            ],
            in_specs=[
                pl.BlockSpec(memory_space=pl.ANY),
                pl.BlockSpec(memory_space=pltpu.VMEM),
                pl.BlockSpec(memory_space=pl.ANY),
                pl.BlockSpec(memory_space=pl.ANY),
            ],
            out_specs=[pl.BlockSpec(memory_space=pl.ANY)] * 6,
            scratch_shapes=[
                pltpu.VMEM((tok, dloc), bf),
                pltpu.VMEM((ny, tok, 128), f32),
                pltpu.VMEM((nx, ny, tok, dloc), bf),
                pltpu.VMEM((2, ny, 2 * krows, tw), bf),
                pltpu.VMEM((nx, SUB, sub, ew), bf),
                pltpu.VMEM((nx, SUB, sub, lw), bf),
                pltpu.VMEM((nx, SUB, ny, sub, ew), bf),
                pltpu.VMEM((nx, SUB, ny, sub, lw), bf),
                pltpu.VMEM((SUB, nx, sub, dloc), f32),
                pltpu.VMEM((2, 2 * tw, dloc), bf),
                pltpu.VMEM((nx - 1, sub, dloc), f32),
                pltpu.VMEM((tok, dloc), bf),
                pltpu.SemaphoreType.DMA((count,)),
                pltpu.SemaphoreType.DMA((count,)),
                pltpu.SemaphoreType.DMA((7,)),
            ],
            compiler_params=pltpu.CompilerParams(
                collective_id=0, has_side_effects=True, vmem_limit_bytes=67043328
            ),
        )(x, gain.reshape(1, dloc), win, wout)
        return outs[0]

    return jax.shard_map(
        local_block,
        mesh=mesh,
        in_specs=(P(("dp", "row"), "col"), P("col"), P("row", "col"), P("row", "col")),
        out_specs=P(("dp", "row"), "col"),
        check_vma=False,
    )
```

time: 899 us -> 454 us (0.51)
  waiting for transfers between devices: 553 us -> 0 us
  Pallas kernels: 0 us -> 451 us
  blocking collectives: 232 us -> 0 us
  matrix products: 76.9 us -> 0 us
  between operations: 13.2 us -> 0.01 us
  other arithmetic: 12.7 us -> 0 us
    pallas_call x0 -> x1, Pallas kernels: none -> 451 us  [local_block(): pl.pallas_call(functools.partial(block, (nx, ny, dloc * ny)), name='mlp_b...]
    reduce_scatter x2 -> x0, waiting for transfers between devices: 373 us -> none  [the longest x1 285 us: local_block(): up_sum = lax.psum_scatter(up_part, 'row', scatter_dimension=0, tiled=True)]
    all_to_all x2 -> x0, blocking collectives: 220 us -> none  [the longest x1 166 us: local_block(): h_cols = lax.all_to_all(h_rows, 'row', 1, 0, tiled=True)]
    all_gather x2 -> x0, waiting for transfers between devices: 179 us -> none  [the longest x1 134 us: local_block(): h_rows = lax.all_gather(h_blk, 'col', axis=1, tiled=True)]
    dot_general x2 -> x0, matrix products: 76.9 us -> none  [the longest x1 38.8 us: local_block(): up_part = jnp.dot(z_cols, w_in_blk, preferred_element_type=jnp.float32)]
    psum x1 -> x0, blocking collectives: 11.8 us -> none  [local_block(): row_stats = lax.psum(part_stats, 'col') / d_model]
    convert_element_type x3 -> x0, other arithmetic: 11 us -> none  [the longest x1 5.56 us: local_block(): h_blk = jax.nn.gelu(up_sum, approximate=True).astype(jnp.bfloat16)]
    all_to_all x2 -> x0, local copies, waits for them, and re-layouts: 10.2 us -> none  [the longest x1 7.53 us: local_block(): h_cols = lax.all_to_all(h_rows, 'row', 1, 0, tiled=True)]
  transfers between devices with their start and end apart: 4 -> 0, of which waited for: 4 -> 0; matrix products, arithmetic and copies ran while one was open for 0% -> 0% of each run, Pallas kernels for 0% -> 0%
where the time goes in v1:
time: 454 us
  Pallas kernels  451 us (99%)
    pallas_call x1, Pallas kernels, local_block(): pl.pallas_call(functools.partial(block, (nx, ny, dloc * ny)), name='mlp_b...  451 us

profile of v1, /device:TPU:96, one launch (start us, length us, event | category | flops | bytes accessed | tf_op | source)
XLA Modules:
  0.0 453.6 jit_solution(16673059721241671502)
XLA Ops:
  0.0 451.3 %mlp_block.1 = (bf16[256,2048]{1,0:T(8,128)(2,1)}, bf16[7,8,1024,256]{3,2,1,0:T(8,128)(2,1)}, bf16[3584,2048]{1,0:T(8,128)(2,1)}, bf16[4,4,64,1024]{3,2,1,0:T(8,...) custom-call(bf16[256,2048]{1,0:T(8,128)(2,1)} %x_hbm.1, f32[1,2048]{1,0:T(1,128)} %bitcast.1, ...), custom_call_target="tpu_custom_call" | custom-call | tf_op jit(solution)/shard_map/mlp_block/pallas_call | solution.py:483
  451.3 2.3 copy.6

commit v2 on v0

v2 whole, which is shorter than its diff:
```python
import functools

import jax
import jax.numpy as jnp
from jax import lax
from jax.experimental import pallas as pl
from jax.experimental.pallas import tpu as pltpu
from jax.sharding import PartitionSpec as P

NORM_EPS = 1e-5
MESH = pl.DeviceIdType.MESH
SUB = 4
LATE = 3


def gelu(v):
    return 0.5 * v * (1.0 + jnp.tanh(0.7978845608028654 * (v + 0.044715 * (v * v * v))))


class Sems:
    def __init__(self):
        self.base, self.total = {}, 0

    def add(self, name, count):
        self.base[name] = self.total
        self.total += count

    def __call__(self, name, index=0):
        return self.base[name] + index


def plan(tiles):
    s = Sems()
    for name, count in (
        ("stat", 3), ("gain", 3), ("mean", 2), ("zx", 4), ("zy", 16), ("w", 3 * tiles), ("wo", tiles), ("wf", 3 * tiles),
        ("wout", 1), ("h1a", 12), ("h1b", 3 * SUB), ("h2a", 12), ("h2b", 3 * SUB), ("aga", 16), ("agb", 4 * SUB), ("y", 6 * SUB),
    ):
        s.add(name, count)
    return s


def block(n, x_hbm, gain_ref, win, wout, y_hbm, w_hbm, wo_hbm, hst_a, hst_b,
          xv, sums, stat, means, gains, z, wt, hm_a, hm_b, hf_a, hf_b, acc, ya, yb, ov, ss, rs, ls):
    nx, ny, d_model = n
    row, cy = lax.axis_index("row"), lax.axis_index("col")
    cx, k = row // 2, lax.rem(row, 2)
    tok, dloc = ov.shape
    tiles, krows, tw = w_hbm.shape[0], w_hbm.shape[2], w_hbm.shape[3]
    early = tiles - LATE
    half = tok // 2
    sub = tok // SUB
    piece = sub // ny
    sem = plan(tiles)

    def ring(v, d, m):
        return lax.rem(v + (d + m), m)

    def dev(dx=0, dy=0, core=None):
        return {"row": 2 * ring(cx, dx, nx) + (k if core is None else core), "col": ring(cy, dy, ny)}

    partner = dev(core=1 - k)

    def remote(src, dst, where, i):
        return pltpu.make_async_remote_copy(
            src_ref=src, dst_ref=dst, send_sem=ss.at[i], recv_sem=rs.at[i], device_id=where, device_id_type=MESH
        )

    sends, z_sends = [], []

    def send(src, dst, where, i, log=sends):
        c = remote(src, dst, where, i)
        c.start()
        log.append(c)

    def got(ref, i):
        remote(ref, ref, partner, i).wait_recv()

    load_x = pltpu.make_async_copy(x_hbm, xv, ls.at[0])
    load_x.start()
    barrier = pltpu.get_barrier_semaphore()
    peers = [partner] + [dev(dx=d) for d in range(1, nx)] + [dev(dy=d) for d in range(1, ny)]
    for p in peers:
        pl.semaphore_signal(barrier, inc=1, device_id=p, device_id_type=MESH)
    load_x.wait()

    lane = lax.broadcasted_iota(jnp.int32, (32, sums.shape[2]), 1)

    def part(i, _):
        at = pl.ds(pl.multiple_of(i * 32, 32), 32)
        v = xv[at, :].astype(jnp.float32)
        s1 = jnp.sum(v, axis=1, keepdims=True)
        s2 = jnp.sum(v * v, axis=1, keepdims=True)
        sums[0, at, :] = jnp.where(lane == 0, s1, s2)
        return 0

    lax.fori_loop(0, tok // 32, part, 0)
    stat[cy] = jnp.transpose(sums[0])[: stat.shape[1]]
    gains[cy] = gain_ref[...]
    pl.semaphore_wait(barrier, len(peers))
    for d in (1, 3, 2):
        send(stat.at[cy], stat.at[cy], dev(dy=d), sem("stat", d - 1))
    for d in (1, 3, 2):
        send(gains.at[cy], gains.at[cy], dev(dy=d), sem("gain", d - 1))

    off = (0, 1, 3, 2)
    lo, hi = pl.ds(0, half), pl.ds(half, half)

    def zb(b, dy, rows=None):
        ref = z.at[ring(cx, off[b], nx), ring(cy, dy, ny)]
        return ref if rows is None else ref.at[rows]

    for d in (1, -1):
        send(xv, zb(0, 0), dev(dy=d), sem("zy", 0 if d == 1 else 1))
    for d in (1, -1):
        send(xv, zb(0, 0), dev(dx=d), sem("zx", 0 if d == 1 else 1))

    def columns(dx, t):
        return pl.ds(pl.multiple_of(ring(cx, dx, nx) * (tiles * tw) + t * tw, 128), tw)

    def w_issue(t):
        for d in (1, 3, 2):
            send(win.at[:, columns(d, t)], w_hbm.at[t, row], dev(dx=d), sem("w", 3 * t + d - 1))
        send(win.at[:, columns(0, t)], w_hbm.at[t, row], partner, sem("wo", t))

    def w_forward(t):
        for d in (1, 3, 2):
            slot = 2 * ring(cx, -d, nx) + k
            got(w_hbm.at[t, slot], sem("w", 3 * t + d - 1))
            send(w_hbm.at[t, slot], w_hbm.at[t, slot], partner, sem("wf", 3 * t + d - 1))

    def w_ready(t):
        got(w_hbm.at[t, row], sem("wo", t))
        for d in (1, 3, 2):
            got(w_hbm.at[t, row], sem("wf", 3 * t + d - 1))

    for d in range(1, ny):
        got(stat.at[0], sem("stat", d - 1))
    total = (stat[0] + stat[1]) + (stat[2] + stat[3])
    mean = total[0:1] / d_model
    rstd = lax.rsqrt(total[1:2] / d_model - mean * mean + NORM_EPS)
    means[0] = jnp.where(lax.broadcasted_iota(jnp.int32, total.shape, 0) == 0, mean, rstd)
    send(means.at[0], means.at[2], dev(dx=1), sem("mean", 0))
    send(means.at[0], means.at[1], dev(dx=-1), sem("mean", 1))
    w_issue(0)
    send(wout, wo_hbm, partner, sem("wout"))

    def spread(b):
        copies = sums.shape[2] // means.shape[1]
        sums[b] = jnp.transpose(jnp.concatenate([means[b]] * copies, axis=0))

    def normalise(b, y, src=None):
        t = ring(cx, off[b], nx)

        def norm(i, _):
            at = pl.ds(pl.multiple_of(i * 32, 32), 32)
            v = (z[t, y, at, :] if src is None else src[at, :]).astype(jnp.float32)
            z[t, y, at, :] = ((v - sums[b, at, 0:1]) * sums[b, at, 1:2] * gains[y]).astype(z.dtype)
            return 0

        lax.fori_loop(0, tok // 32, norm, 0)

    spread(0)
    normalise(0, cy, xv)

    up_y, down_y, far_y = ring(cy, 1, ny), ring(cy, -1, ny), ring(cy, 2, ny)

    def zx_forward():
        got(xv, sem("zx", 0))
        got(means.at[0], sem("mean", 0))
        spread(2)
        normalise(2, cy)
        send(zb(2, 0, lo), zb(2, 0, lo), dev(dx=1), sem("zx", 2), z_sends)
        zy_send(2)
        got(xv, sem("zx", 1))
        got(means.at[0], sem("mean", 1))
        spread(1)
        normalise(1, cy)
        send(zb(1, 0, hi), zb(1, 0, hi), dev(dx=-1), sem("zx", 3), z_sends)
        zy_send(1)

    def zx_last():
        got(zb(3, 0, lo), sem("zx", 2))
        got(zb(3, 0, hi), sem("zx", 3))

    def zy_send(b):
        send(zb(b, 0), zb(b, 0), dev(dy=1), sem("zy", 4 * b), z_sends)
        send(zb(b, 0), zb(b, 0), dev(dy=-1), sem("zy", 4 * b + 1), z_sends)

    def zy_forward(b):
        got(zb(b, -1), sem("zy", 4 * b))
        send(zb(b, -1, lo), zb(b, -1, lo), dev(dy=1), sem("zy", 4 * b + 2), z_sends)
        got(zb(b, 1), sem("zy", 4 * b + 1))
        send(zb(b, 1, hi), zb(b, 1, hi), dev(dy=-1), sem("zy", 4 * b + 3), z_sends)

    def zy_last(b):
        got(zb(b, 2, lo), sem("zy", 4 * b + 2))
        got(zb(b, 2, hi), sem("zy", 4 * b + 3))

    def zy_forward_own():
        got(xv, sem("zy", 0))
        for d in range(1, ny):
            got(gains.at[0], sem("gain", d - 1))
        normalise(0, down_y)
        send(zb(0, -1, lo), zb(0, -1, lo), dev(dy=1), sem("zy", 2), z_sends)
        got(xv, sem("zy", 1))
        normalise(0, up_y)
        send(zb(0, 1, hi), zb(0, 1, hi), dev(dy=-1), sem("zy", 3), z_sends)

    def wt_load(t, slot):
        for j in range(2 * nx):
            r = ring(row, j, 2 * nx)
            dst = wt.at[slot, r // 2, pl.ds(pl.multiple_of(lax.rem(r, 2) * krows, krows), krows)]
            src = win.at[:, columns(0, t)] if j == 0 else w_hbm.at[t, r]
            pltpu.make_async_copy(src, dst, ls.at[1 + slot]).start()

    def wt_wait(slot):
        pltpu.make_async_copy(wt.at[slot], wt.at[slot], ls.at[1 + slot]).wait()

    def up_load(t0, t1):
        for i in range(min(2, t1 - t0)):
            wt_load(t0 + i, i)

    def up(late, t0, t1, b0, b1, loaded=False):
        hm, hf, first = (hm_b, hf_b, early) if late else (hm_a, hf_a, 0)
        if not loaded:
            up_load(t0, t1)

        def tile(i, _):
            slot = lax.rem(i, 3)
            wt_wait(slot)

            @pl.when(i + 2 < t1 - t0)
            def _():
                wt_load(t0 + i + 2, lax.rem(i + 2, 3))

            at = pl.ds(pl.multiple_of((t0 + i - first) * tw, 128), tw)

            def rows(b, _):
                t = ring(cx, b + b // 2 - 2 * (b // 3), nx)
                v = jnp.dot(z[t, 0], wt[slot, 0], preferred_element_type=jnp.float32)
                for j in range(1, ny):
                    v += jnp.dot(z[t, j], wt[slot, j], preferred_element_type=jnp.float32)
                hm[t, :, :, :, at] = gelu(v).astype(hm.dtype).reshape(ny, SUB, piece, tw)

                @pl.when(cx == cy)
                def _():
                    hf[cx, :, t, cy, :, at] = hm[t, cy, :, :, at]

                return 0

            lax.fori_loop(b0, b1, rows, 0)
            return 0

        lax.fori_loop(0, t1 - t0, tile, 0)

    def h1_a(b):
        t = ring(cx, off[b], nx)
        for d in (1, 3, 2):
            c = ring(cy, d, ny)
            i = sem("h1a", 3 * b + d - 1)

            @pl.when(cx == cy)
            def _():
                remote(hm_a.at[t, c], hf_a.at[cx, :, t, c], dev(dy=d), i).start()

            @pl.when(cx != cy)
            def _():
                remote(hm_a.at[t, c], hst_a.at[cy, :, t], dev(dy=d), i).start()

            sends.append(remote(hm_a.at[t, c], hst_a.at[cy, :, t], dev(dy=d), i))

    def h2_a(b):
        t = ring(cx, off[b], nx)
        for d in range(1, ny):
            got(hst_a.at[0, :, 0], sem("h1a", 3 * b + d - 1))
        for d in (1, 3, 2):
            c = ring(cx, d, nx)
            i = sem("h2a", 3 * b + d - 1)

            @pl.when(c == cy)
            def _():
                remote(hm_a.at[t, cy], hf_a.at[cx, :, t, cy], dev(dx=d), i).start()

            @pl.when(c != cy)
            def _():
                remote(hst_a.at[c, :, t], hf_a.at[cx, :, t, cy], dev(dx=d), i).start()

            sends.append(remote(hst_a.at[c, :, t], hf_a.at[cx, :, t, cy], dev(dx=d), i))

    def h1_b(s):
        for d in (1, 3, 2):
            c = ring(cy, d, ny)
            i = sem("h1b", 3 * s + d - 1)

            @pl.when(cx == cy)
            def _():
                remote(hm_b.at[:, c, s], hf_b.at[cx, s, :, c], dev(dy=d), i).start()

            @pl.when(cx != cy)
            def _():
                remote(hm_b.at[:, c, s], hst_b.at[cy, s], dev(dy=d), i).start()

            sends.append(remote(hm_b.at[:, c, s], hst_b.at[cy, s], dev(dy=d), i))

    def h2_b(s):
        for d in range(1, ny):
            got(hst_b.at[0, 0], sem("h1b", 3 * s + d - 1))
        for d in (1, 3, 2):
            c = ring(cx, d, nx)
            i = sem("h2b", 3 * s + d - 1)

            @pl.when(c == cy)
            def _():
                remote(hm_b.at[:, cy, s], hf_b.at[cx, s, :, cy], dev(dx=d), i).start()

            @pl.when(c != cy)
            def _():
                remote(hst_b.at[c, s], hf_b.at[cx, s, :, cy], dev(dx=d), i).start()

            sends.append(remote(hst_b.at[c, s], hf_b.at[cx, s, :, cy], dev(dx=d), i))

    x_low, x_high = pl.ds(0, nx // 2), pl.ds(nx // 2, nx // 2)

    def gather(name, index, part):
        everything = pl.ds(0, nx)
        i = sem(name, 4 * index)

        def begin():
            send(part(everything, cy), part(everything, cy), dev(dy=1), i)
            send(part(everything, cy), part(everything, cy), dev(dy=-1), i + 1)

        def forward():
            got(part(everything, cy), i)
            send(part(x_low, down_y), part(x_low, down_y), dev(dy=1), i + 2)
            got(part(everything, cy), i + 1)
            send(part(x_high, up_y), part(x_high, up_y), dev(dy=-1), i + 3)

        def last():
            got(part(x_low, far_y), i + 2)
            got(part(x_high, far_y), i + 3)

        return begin, forward, last

    gather_a = [gather("aga", b, lambda c, y, b=b: hf_a.at[c, :, ring(cx, off[b], nx), y]) for b in range(nx)]
    gather_b = [gather("agb", s, lambda c, y, s=s: hf_b.at[c, s, :, y]) for s in range(SUB)]

    def ag_a(b):
        for d in range(1, nx):
            got(hst_a.at[0, :, 0], sem("h2a", 3 * off.index((off[b] + d) % nx) + d - 1))
        gather_a[b][0]()

    def ag_a_forward(b):
        gather_a[b][1]()

    def ag_a_last(b):
        gather_a[b][2]()

    def ag_b(s):
        for d in range(1, nx):
            got(hst_b.at[0, 0], sem("h2b", 3 * s + d - 1))
        gather_b[s][0]()

    def ag_b_forward(s):
        gather_b[s][1]()

    def ag_b_last(s):
        gather_b[s][2]()

    ew, lw = early * tw, LATE * tw
    npt = 2 * krows // ew
    steps = dloc // (npt * tw)
    kept = lw // tok

    def rows_of(c, skip, count, use):
        at = pl.ds(pl.multiple_of(lax.rem(c, 2) * (ew + lw) + skip, 128), count)

        @pl.when(c // 2 == k)
        def _():
            use(wout, at)

        @pl.when(c // 2 != k)
        def _():
            use(wo_hbm, at)

    def we_load(i, slot):
        for c in range(nx):
            for j in range(npt):
                cols = pl.ds(pl.multiple_of((i * npt + j) * tw, 128), tw)
                dst = wt.at[slot, c, pl.ds(j * ew, ew)]
                rows_of(c, 0, ew, lambda ref, at: pltpu.make_async_copy(ref.at[at, cols], dst, ls.at[1 + slot]).start())

    def we_wait(slot):
        ref = wt.at[slot, :, pl.ds(0, npt * ew)]
        pltpu.make_async_copy(ref, ref, ls.at[1 + slot]).wait()

    def down_early_load():
        for i in range(min(2, steps)):
            we_load(i, i)

    def down_early(b0, b1, loaded=False):
        if not loaded:
            down_early_load()

        def step(i, _):
            slot = lax.rem(i, 3)
            we_wait(slot)

            @pl.when(i + 2 < steps)
            def _():
                we_load(i + 2, lax.rem(i + 2, 3))

            def rows(b, _):
                t = ring(cx, b + b // 2 - 2 * (b // 3), nx)
                for j in range(npt):
                    v = None
                    for c in range(nx):
                        h = hf_a[c, :, t].reshape(tok, ew)
                        p = jnp.dot(h, wt[slot, c, pl.ds(j * ew, ew)], preferred_element_type=jnp.float32)
                        v = p if v is None else v + p
                    cols = pl.ds(pl.multiple_of((i * npt + j) * tw, 128), tw)
                    acc[:, t, :, cols] = v.reshape(SUB, sub, tw)
                return 0

            lax.fori_loop(b0, b1, rows, 0)
            return 0

        lax.fori_loop(0, steps, step, 0)

    def late_start():
        for c in z_sends:
            c.wait_send()
        for c in range(nx):
            for j in range(kept):
                rows_of(c, ew + j * tok, tok, lambda ref, at: pltpu.make_async_copy(ref.at[at], z.at[c, j], ls.at[4]).start())

    def late_wait():
        ref = z.at[:, pl.ds(0, kept)]
        pltpu.make_async_copy(ref, ref, ls.at[4]).wait()

    def down_late(s):
        wide = 2 * tw

        def step(i, _):
            cols = pl.ds(pl.multiple_of(i * wide, 128), wide)
            v = None
            for c in range(nx):
                h = hf_b[c, s].reshape(nx * sub, lw)
                p = jnp.dot(h, z[c, pl.ds(0, kept), :, cols].reshape(lw, wide), preferred_element_type=jnp.float32)
                v = p if v is None else v + p
            acc[s, :, :, cols] += v.reshape(nx, sub, wide)
            return 0

        lax.fori_loop(0, dloc // wide, step, 0)

    top, low = pl.ds(0, sub // 2), pl.ds(sub // 2, sub // 2)
    right, left, across = ring(cx, 1, nx), ring(cx, -1, nx), ring(cx, 2, nx)

    def y_send(s):
        send(acc.at[s, across, top], ya.at[s, 0], dev(dx=1), sem("y", 6 * s))
        send(acc.at[s, across, low], ya.at[s, 1], dev(dx=-1), sem("y", 6 * s + 1))
        send(acc.at[s, right, low], yb.at[s, 0, low], dev(dx=1), sem("y", 6 * s + 2))
        send(acc.at[s, left, top], yb.at[s, 1, top], dev(dx=-1), sem("y", 6 * s + 3))

    def y_forward(s):
        got(ya.at[s, 0], sem("y", 6 * s))
        acc[s, right, top] += ya[s, 0]
        send(acc.at[s, right, top], yb.at[s, 0, top], dev(dx=1), sem("y", 6 * s + 4))
        got(ya.at[s, 1], sem("y", 6 * s + 1))
        acc[s, left, low] += ya[s, 1]
        send(acc.at[s, left, low], yb.at[s, 1, low], dev(dx=-1), sem("y", 6 * s + 5))

    def y_final(s):
        for j in range(2, 6):
            got(ya.at[s, 0], sem("y", 6 * s + j))
        for c in range(ny):
            rows, at = pl.ds(c * piece, piece), pl.ds(c * sub + s * piece, piece)
            total = acc[s, cx, rows] + (yb[s, 0, rows] + yb[s, 1, rows])
            ov[at, :] = (xv[at, :].astype(jnp.float32) + total).astype(ov.dtype)

    n0, n1, n2, n3, n4, n5, n6, n7 = range(8)
    zy_forward_own()
    zx_forward()
    w_issue(n1)
    w_issue(n2)
    w_issue(n3)
    w_issue(n4)
    w_forward(n0)
    zy_forward(n2)
    zx_last()
    zy_send(n3)
    w_forward(n1)
    w_forward(n2)
    zy_last(n0)
    w_ready(n1)
    up(n0, n1, n2, n0, n1)
    w_ready(n0)
    up(n0, n0, n1, n0, n1)
    zy_last(n2)
    w_ready(n2)
    up(n0, n2, n3, n0, n1)
    zy_forward(n1)
    up(n0, n0, n3, n2, n3)
    w_forward(n3)
    zy_forward(n3)
    zy_last(n1)
    w_ready(n3)
    up(n0, n3, n4, n0, n3)
    h1_a(n2)
    h1_a(n0)
    zy_last(n3)
    up(n0, n0, n4, n3, n4)
    h2_a(n2)
    h1_a(n3)
    h2_a(n0)
    up(n0, n0, n3, n1, n2)
    h1_a(n1)
    h2_a(n3)
    h2_a(n1)
    ag_a(n1)
    w_issue(n5)
    ag_a(n0)
    w_forward(n4)
    w_ready(n4)
    up(n1, n4, n5, n0, n4)
    w_issue(n6)
    ag_a(n3)
    ag_a_forward(n1)
    w_forward(n5)
    ag_a_forward(n3)
    w_ready(n5)
    up(n1, n5, n6, n0, n4)
    ag_a(n2)
    w_forward(n6)
    ag_a_last(n3)
    ag_a_forward(n0)
    got(wo_hbm, sem("wout"))
    down_early(n3, n4)
    ag_a_forward(n2)
    w_ready(n6)
    up(n1, n6, n7, n0, n4)
    h1_b(n0)
    h1_b(n1)
    ag_a_last(n0)
    down_early(n0, n1)
    h2_b(n0)
    ag_a_last(n1)
    ag_a_last(n2)
    h1_b(n2)
    late_start()
    h2_b(n1)
    ag_b(n0)
    down_early(n2, n3)
    h1_b(n3)
    h2_b(n2)
    ag_b_forward(n0)
    down_early(n1, n2)
    late_wait()
    h2_b(n3)
    ag_b(n1)
    ag_b_last(n0)
    down_late(n0)
    y_send(n0)
    ag_b_forward(n1)
    y_forward(n0)
    ag_b(n2)
    ag_b_last(n1)
    down_late(n1)
    y_send(n1)
    ag_b_forward(n2)
    y_forward(n1)
    ag_b_last(n2)
    ag_b(n3)
    down_late(n2)
    y_send(n2)
    y_final(n0)
    ag_b_forward(n3)
    y_forward(n2)
    ag_b_last(n3)
    down_late(n3)
    y_send(n3)
    y_final(n1)
    y_final(n2)
    y_forward(n3)
    y_final(n3)
    out = pltpu.make_async_copy(ov, y_hbm, ls.at[0])
    out.start()
    for c in sends:
        c.wait_send()
    out.wait()


def solution(mesh):
    nx, ny = mesh.shape["row"] // 2, mesh.shape["col"]

    def local_block(x, gain, win, wout):
        tok, dloc = x.shape
        krows, floc = win.shape
        width = floc // nx
        tw = width // 7
        tiles = width // tw
        early = tiles - LATE
        ew, lw = early * tw, LATE * tw
        sub = tok // SUB
        piece = sub // ny
        bf, f32 = jnp.bfloat16, jnp.float32
        count = plan(tiles).total
        hbm = lambda shape, dt: jax.ShapeDtypeStruct(shape, dt)
        outs = pl.pallas_call(
            functools.partial(block, (nx, ny, dloc * ny)),
            name="mlp_block",
            out_shape=[
                hbm((tok, dloc), bf),
                hbm((tiles, 2 * nx, krows, tw), bf),
                hbm(wout.shape, bf),
                hbm((ny, SUB, nx, piece, ew), bf),
                hbm((ny, SUB, nx, piece, lw), bf),
            ],
            in_specs=[
                pl.BlockSpec(memory_space=pl.ANY),
                pl.BlockSpec(memory_space=pltpu.VMEM),
                pl.BlockSpec(memory_space=pl.ANY),
                pl.BlockSpec(memory_space=pl.ANY),
            ],
            out_specs=[pl.BlockSpec(memory_space=pl.ANY)] * 5,
            scratch_shapes=[
                pltpu.VMEM((tok, dloc), bf),
                pltpu.VMEM((3, tok, 128), f32),
                pltpu.VMEM((ny, 8, tok), f32),
                pltpu.VMEM((3, 8, tok), f32),
                pltpu.VMEM((ny, 1, dloc), f32),
                pltpu.VMEM((nx, ny, tok, dloc), bf),
                pltpu.VMEM((3, ny, 2 * krows, tw), bf),
                pltpu.VMEM((nx, ny, SUB, piece, ew), bf),
                pltpu.VMEM((nx, ny, SUB, piece, lw), bf),
                pltpu.VMEM((nx, SUB, nx, ny, piece, ew), bf),
                pltpu.VMEM((nx, SUB, nx, ny, piece, lw), bf),
                pltpu.VMEM((SUB, nx, sub, dloc), f32),
                pltpu.VMEM((SUB, 2, sub // 2, dloc), f32),
                pltpu.VMEM((SUB, 2, sub, dloc), f32),
                pltpu.VMEM((tok, dloc), bf),
                pltpu.SemaphoreType.DMA((count,)),
                pltpu.SemaphoreType.DMA((count,)),
                pltpu.SemaphoreType.DMA((5,)),
            ],
            compiler_params=pltpu.CompilerParams(
                collective_id=0, has_side_effects=True, vmem_limit_bytes=67043328
            ),
        )(x, gain.reshape(1, dloc), win, wout)
        return outs[0]

    return jax.shard_map(
        local_block,
        mesh=mesh,
        in_specs=(P(("dp", "row"), "col"), P("col"), P("row", "col"), P("row", "col")),
        out_specs=P(("dp", "row"), "col"),
        check_vma=False,
    )
```

time: 899 us -> 353 us (0.39)
  waiting for transfers between devices: 553 us -> 0 us
  Pallas kernels: 0 us -> 348 us
  blocking collectives: 232 us -> 0 us
  matrix products: 76.9 us -> 0 us
  between operations: 13.2 us -> 0.01 us
  other arithmetic: 12.7 us -> 0 us
    reduce_scatter x2 -> x0, waiting for transfers between devices: 373 us -> none  [the longest x1 285 us: local_block(): up_sum = lax.psum_scatter(up_part, 'row', scatter_dimension=0, tiled=True)]
    pallas_call x0 -> x1, Pallas kernels: none -> 348 us  [local_block(): pl.pallas_call(functools.partial(block, (nx, ny, dloc * ny)), name='mlp_b...]
    all_to_all x2 -> x0, blocking collectives: 220 us -> none  [the longest x1 166 us: local_block(): h_cols = lax.all_to_all(h_rows, 'row', 1, 0, tiled=True)]
    all_gather x2 -> x0, waiting for transfers between devices: 179 us -> none  [the longest x1 134 us: local_block(): h_rows = lax.all_gather(h_blk, 'col', axis=1, tiled=True)]
    dot_general x2 -> x0, matrix products: 76.9 us -> none  [the longest x1 38.8 us: local_block(): up_part = jnp.dot(z_cols, w_in_blk, preferred_element_type=jnp.float32)]
    psum x1 -> x0, blocking collectives: 11.8 us -> none  [local_block(): row_stats = lax.psum(part_stats, 'col') / d_model]
    convert_element_type x3 -> x0, other arithmetic: 11 us -> none  [the longest x1 5.56 us: local_block(): h_blk = jax.nn.gelu(up_sum, approximate=True).astype(jnp.bfloat16)]
    all_to_all x2 -> x0, local copies, waits for them, and re-layouts: 10.2 us -> none  [the longest x1 7.53 us: local_block(): h_cols = lax.all_to_all(h_rows, 'row', 1, 0, tiled=True)]
  transfers between devices with their start and end apart: 4 -> 0, of which waited for: 4 -> 0; matrix products, arithmetic and copies ran while one was open for 0% -> 0% of each run, Pallas kernels for 0% -> 0%
where the time goes in v2:
time: 353 us; the launch traced here: 351 us
  Pallas kernels  348 us (99%)
    pallas_call x1, Pallas kernels, local_block(): pl.pallas_call(functools.partial(block, (nx, ny, dloc * ny)), name='mlp_b...  348 us

profile of v2, /device:TPU:96, one launch (start us, length us, event | category | flops | bytes accessed | tf_op | source)
XLA Modules:
  0.0 350.6 jit_solution(2706889661001635753)
XLA Ops:
  0.0 348.3 %mlp_block.1 = (bf16[256,2048]{1,0:T(8,128)(2,1)}, bf16[7,8,1024,256]{3,2,1,0:T(8,128)(2,1)}, bf16[3584,2048]{1,0:T(8,128)(2,1)}, bf16[4,4,4,16,1024]{4,3,2,1,0:T(8,128)(2,1)}, bf16[4,4,4,16,768]{4,3,2,1,0:T(8,128)(2,1)}) custom-call(bf16[256,2048]{1,0:T(8,128)(2,1)} %x_hbm.1, f32[1,2048]{1,0:T(1,128)} %bitcast.1, bf16[1024,7168]{1,0:T(8,128)(2,1)} %win.1, ...), custom_call_target="tpu_custom_call" | custom-call | tf_op jit(solution)/shard_map/mlp_block/pallas_call | solution.py:608
  348.3 2.3 copy.6

commit v3 on v2

--- a/solution.py
+++ b/solution.py
@@ -9,7 +9,8 @@
 
 NORM_EPS = 1e-5
 MESH = pl.DeviceIdType.MESH
-SUB = 4
+SUB = 8
+GROUPS = 4
 LATE = 3
 
 
@@ -33,14 +34,15 @@
     s = Sems()
     for name, count in (
         ("stat", 3), ("gain", 3), ("mean", 2), ("zx", 4), ("zy", 16), ("w", 3 * tiles), ("wo", tiles), ("wf", 3 * tiles),
-        ("wout", 1), ("h1a", 12), ("h1b", 3 * SUB), ("h2a", 12), ("h2b", 3 * SUB), ("aga", 16), ("agb", 4 * SUB), ("y", 6 * SUB),
+        ("wout", 1), ("h1a", 12), ("h1b", 3 * SUB), ("h2a", 12 * GROUPS), ("h2b", 3 * SUB),
+        ("own", 16), ("aga", 4 * GROUPS), ("agb", 4 * SUB), ("y", 6 * SUB),
     ):
         s.add(name, count)
     return s
 
 
 def block(n, x_hbm, gain_ref, win, wout, y_hbm, w_hbm, wo_hbm, hst_a, hst_b,
-          xv, sums, stat, means, gains, z, wt, hm_a, hm_b, hf_a, hf_b, acc, ya, yb, ov, ss, rs, ls):
+          xv, sums, stat, means, gains, z, wt, hm_a, hm_b, hf_a, hf_b, acc, pre, ya, yb, ov, ss, rs, ls):
     nx, ny, d_model = n
     row, cy = lax.axis_index("row"), lax.axis_index("col")
     cx, k = row // 2, lax.rem(row, 2)
@@ -50,6 +52,7 @@
     half = tok // 2
     sub = tok // SUB
     piece = sub // ny
+    batch = SUB // GROUPS
     sem = plan(tiles)
 
     def ring(v, d, m):
@@ -122,16 +125,28 @@
             send(win.at[:, columns(d, t)], w_hbm.at[t, row], dev(dx=d), sem("w", 3 * t + d - 1))
         send(win.at[:, columns(0, t)], w_hbm.at[t, row], partner, sem("wo", t))
 
-    def w_forward(t):
-        for d in (1, 3, 2):
+    def w_pass(t, ds):
+        for d in ds:
             slot = 2 * ring(cx, -d, nx) + k
             got(w_hbm.at[t, slot], sem("w", 3 * t + d - 1))
             send(w_hbm.at[t, slot], w_hbm.at[t, slot], partner, sem("wf", 3 * t + d - 1))
 
+    def w_got(t, ds):
+        for d in ds:
+            got(w_hbm.at[t, row], sem("wf", 3 * t + d - 1))
+
+    def w_forward(t):
+        w_pass(t, (1, 3, 2))
+
     def w_ready(t):
         got(w_hbm.at[t, row], sem("wo", t))
-        for d in (1, 3, 2):
-            got(w_hbm.at[t, row], sem("wf", 3 * t + d - 1))
+        w_got(t, (1, 3, 2))
+
+    def w_forward_near(t):
+        w_pass(t, (1, 3))
+
+    def w_forward_far(t):
+        w_pass(t, (2,))
 
     for d in range(1, ny):
         got(stat.at[0], sem("stat", d - 1))
@@ -206,12 +221,16 @@
         normalise(0, up_y)
         send(zb(0, 1, hi), zb(0, 1, hi), dev(dy=-1), sem("zy", 3), z_sends)
 
+    def wt_rows(t, slot, rows):
+        for j in rows:
+            for core in range(2):
+                r = 2 * ring(cx, j, nx) + lax.rem(k + core, 2)
+                dst = wt.at[slot, r // 2, pl.ds(pl.multiple_of(lax.rem(r, 2) * krows, krows), krows)]
+                src = win.at[:, columns(0, t)] if j == 0 and core == 0 else w_hbm.at[t, r]
+                pltpu.make_async_copy(src, dst, ls.at[1 + slot]).start()
+
     def wt_load(t, slot):
-        for j in range(2 * nx):
-            r = ring(row, j, 2 * nx)
-            dst = wt.at[slot, r // 2, pl.ds(pl.multiple_of(lax.rem(r, 2) * krows, krows), krows)]
-            src = win.at[:, columns(0, t)] if j == 0 else w_hbm.at[t, r]
-            pltpu.make_async_copy(src, dst, ls.at[1 + slot]).start()
+        wt_rows(t, slot, range(nx))
 
     def wt_wait(slot):
         pltpu.make_async_copy(wt.at[slot], wt.at[slot], ls.at[1 + slot]).wait()
@@ -244,7 +263,7 @@
 
                 @pl.when(cx == cy)
                 def _():
-                    hf[cx, :, t, cy, :, at] = hm[t, cy, :, :, at]
+                    hf[0, :, t, cy, :, at] = hm[t, cy, :, :, at]
 
                 return 0
 
@@ -252,6 +271,43 @@
             return 0
 
         lax.fori_loop(0, t1 - t0, tile, 0)
+
+    def up_near(t):
+        got(w_hbm.at[t, row], sem("wo", t))
+        w_got(t, (1, 3))
+        wt_rows(t, 0, (0, 1, 3))
+        ref = wt.at[0, pl.ds(0, ny - 1)]
+        pltpu.make_async_copy(ref, ref, ls.at[1]).wait()
+
+        def rows(b, _):
+            v = None
+            for j in (0, 1, 3):
+                f = ring(cx, j, nx)
+                p = jnp.dot(z[b, f], wt[0, f], preferred_element_type=jnp.float32)
+                v = p if v is None else v + p
+            pre[b] = v
+            return 0
+
+        lax.fori_loop(0, nx, rows, 0)
+
+    def up_far(t):
+        w_got(t, (2,))
+        wt_rows(t, 0, (2,))
+        f = ring(cx, 2, nx)
+        pltpu.make_async_copy(wt.at[0, f], wt.at[0, f], ls.at[1]).wait()
+        at = pl.ds((t - early) * tw, tw)
+
+        def rows(b, _):
+            v = pre[b] + jnp.dot(z[b, f], wt[0, f], preferred_element_type=jnp.float32)
+            hm_b[b, :, :, :, at] = gelu(v).astype(hm_b.dtype).reshape(ny, SUB, piece, tw)
+
+            @pl.when(cx == cy)
+            def _():
+                hf_b[0, :, b, cy, :, at] = hm_b[b, cy, :, :, at]
+
+            return 0
+
+        lax.fori_loop(0, nx, rows, 0)
 
     def h1_a(b):
         t = ring(cx, off[b], nx)
@@ -261,7 +317,7 @@
 
             @pl.when(cx == cy)
             def _():
-                remote(hm_a.at[t, c], hf_a.at[cx, :, t, c], dev(dy=d), i).start()
+                remote(hm_a.at[t, c], hf_a.at[0, :, t, c], dev(dy=d), i).start()
 
             @pl.when(cx != cy)
             def _():
@@ -269,23 +325,26 @@
 
             sends.append(remote(hm_a.at[t, c], hst_a.at[cy, :, t], dev(dy=d), i))
 
-    def h2_a(b):
-        t = ring(cx, off[b], nx)
+    def h1_wait(b):
         for d in range(1, ny):
             got(hst_a.at[0, :, 0], sem("h1a", 3 * b + d - 1))
+
+    def h2_a(b, g):
+        t = ring(cx, off[b], nx)
+        some = pl.ds(g * batch, batch)
         for d in (1, 3, 2):
             c = ring(cx, d, nx)
-            i = sem("h2a", 3 * b + d - 1)
+            i = sem("h2a", 12 * g + 3 * b + d - 1)
 
             @pl.when(c == cy)
             def _():
-                remote(hm_a.at[t, cy], hf_a.at[cx, :, t, cy], dev(dx=d), i).start()
+                remote(hm_a.at[t, cy, some], hf_a.at[nx - d, some, t, cy], dev(dx=d), i).start()
 
             @pl.when(c != cy)
             def _():
-                remote(hst_a.at[c, :, t], hf_a.at[cx, :, t, cy], dev(dx=d), i).start()
-
-            sends.append(remote(hst_a.at[c, :, t], hf_a.at[cx, :, t, cy], dev(dx=d), i))
+                remote(hst_a.at[c, some, t], hf_a.at[nx - d, some, t, cy], dev(dx=d), i).start()
+
+            sends.append(remote(hst_a.at[c, some, t], hf_a.at[nx - d, some, t, cy], dev(dx=d), i))
 
     def h1_b(s):
         for d in (1, 3, 2):
@@ -294,7 +353,7 @@
 
             @pl.when(cx == cy)
             def _():
-                remote(hm_b.at[:, c, s], hf_b.at[cx, s, :, c], dev(dy=d), i).start()
+                remote(hm_b.at[:, c, s], hf_b.at[0, s, :, c], dev(dy=d), i).start()
 
             @pl.when(cx != cy)
             def _():
@@ -311,60 +370,78 @@
 
             @pl.when(c == cy)
             def _():
-                remote(hm_b.at[:, cy, s], hf_b.at[cx, s, :, cy], dev(dx=d), i).start()
+                remote(hm_b.at[:, cy, s], hf_b.at[nx - d, s, :, cy], dev(dx=d), i).start()
 
             @pl.when(c != cy)
             def _():
-                remote(hst_b.at[c, s], hf_b.at[cx, s, :, cy], dev(dx=d), i).start()
-
-            sends.append(remote(hst_b.at[c, s], hf_b.at[cx, s, :, cy], dev(dx=d), i))
-
-    x_low, x_high = pl.ds(0, nx // 2), pl.ds(nx // 2, nx // 2)
-
-    def gather(name, index, part):
-        everything = pl.ds(0, nx)
-        i = sem(name, 4 * index)
-
+                remote(hst_b.at[c, s], hf_b.at[nx - d, s, :, cy], dev(dx=d), i).start()
+
+            sends.append(remote(hst_b.at[c, s], hf_b.at[nx - d, s, :, cy], dev(dx=d), i))
+
+    def gather(i, whole, low, high):
         def begin():
-            send(part(everything, cy), part(everything, cy), dev(dy=1), i)
-            send(part(everything, cy), part(everything, cy), dev(dy=-1), i + 1)
+            send(whole(cy), whole(cy), dev(dy=1), i)
+            send(whole(cy), whole(cy), dev(dy=-1), i + 1)
 
         def forward():
-            got(part(everything, cy), i)
-            send(part(x_low, down_y), part(x_low, down_y), dev(dy=1), i + 2)
-            got(part(everything, cy), i + 1)
-            send(part(x_high, up_y), part(x_high, up_y), dev(dy=-1), i + 3)
+            got(whole(cy), i)
+            send(low(down_y), low(down_y), dev(dy=1), i + 2)
+            got(whole(cy), i + 1)
+            send(high(up_y), high(up_y), dev(dy=-1), i + 3)
 
         def last():
-            got(part(x_low, far_y), i + 2)
-            got(part(x_high, far_y), i + 3)
+            got(low(far_y), i + 2)
+            got(high(far_y), i + 3)
 
         return begin, forward, last
 
-    gather_a = [gather("aga", b, lambda c, y, b=b: hf_a.at[c, :, ring(cx, off[b], nx), y]) for b in range(nx)]
-    gather_b = [gather("agb", s, lambda c, y, s=s: hf_b.at[c, s, :, y]) for s in range(SUB)]
-
-    def ag_a(b):
-        for d in range(1, nx):
-            got(hst_a.at[0, :, 0], sem("h2a", 3 * off.index((off[b] + d) % nx) + d - 1))
-        gather_a[b][0]()
-
-    def ag_a_forward(b):
-        gather_a[b][1]()
-
-    def ag_a_last(b):
-        gather_a[b][2]()
+    def gather_own(b):
+        t = ring(cx, off[b], nx)
+        part = lambda s, n: lambda y: hf_a.at[0, pl.ds(s, n), t, y]
+        return gather(sem("own", 4 * b), part(0, SUB), part(0, SUB // 2), part(SUB // 2, SUB // 2))
+
+    def gather_a(g):
+        part = lambda s, n: lambda y: hf_a.at[pl.ds(1, nx - 1), pl.ds(g * batch + s, n), :, y]
+        return gather(sem("aga", 4 * g), part(0, batch), part(0, batch // 2), part(batch // 2, batch // 2))
+
+    def gather_b(s):
+        part = lambda c, n: lambda y: hf_b.at[pl.ds(c, n), s, :, y]
+        return gather(sem("agb", 4 * s), part(0, nx), part(0, nx // 2), part(nx // 2, nx // 2))
+
+    own_gathers = [gather_own(b) for b in range(nx)]
+    a_gathers = [gather_a(g) for g in range(GROUPS)]
+    b_gathers = [gather_b(s) for s in range(SUB)]
+
+    def own_a(b):
+        own_gathers[b][0]()
+
+    def own_a_forward(b):
+        own_gathers[b][1]()
+
+    def own_a_last(b):
+        own_gathers[b][2]()
+
+    def ag_a(g):
+        for j in range(12):
+            got(hst_a.at[0, pl.ds(0, batch), 0], sem("h2a", 12 * g + j))
+        a_gathers[g][0]()
+
+    def ag_a_forward(g):
+        a_gathers[g][1]()
+
+    def ag_a_last(g):
+        a_gathers[g][2]()
 
     def ag_b(s):
         for d in range(1, nx):
             got(hst_b.at[0, 0], sem("h2b", 3 * s + d - 1))
-        gather_b[s][0]()
+        b_gathers[s][0]()
 
     def ag_b_forward(s):
-        gather_b[s][1]()
+        b_gathers[s][1]()
 
     def ag_b_last(s):
-        gather_b[s][2]()
+        b_gathers[s][2]()
 
     ew, lw = early * tw, LATE * tw
     npt = 2 * krows // ew
@@ -383,11 +460,11 @@
             use(wo_hbm, at)
 
     def we_load(i, slot):
-        for c in range(nx):
-            for j in range(npt):
+        for j in range(npt):
+            for p in range(nx):
                 cols = pl.ds(pl.multiple_of((i * npt + j) * tw, 128), tw)
-                dst = wt.at[slot, c, pl.ds(j * ew, ew)]
-                rows_of(c, 0, ew, lambda ref, at: pltpu.make_async_copy(ref.at[at, cols], dst, ls.at[1 + slot]).start())
+                dst = wt.at[slot, p, pl.ds(j * ew, ew)]
+                rows_of(ring(cx, p, nx), 0, ew, lambda ref, at: pltpu.make_async_copy(ref.at[at, cols], dst, ls.at[1 + slot]).start())
 
     def we_wait(slot):
         ref = wt.at[slot, :, pl.ds(0, npt * ew)]
@@ -397,7 +474,8 @@
         for i in range(min(2, steps)):
             we_load(i, i)
 
-    def down_early(b0, b1, loaded=False):
+    def down_early(g, loaded=False):
+        some = pl.ds(g * batch, batch)
         if not loaded:
             down_early_load()
 
@@ -409,19 +487,14 @@
             def _():
                 we_load(i + 2, lax.rem(i + 2, 3))
 
-            def rows(b, _):
-                t = ring(cx, b + b // 2 - 2 * (b // 3), nx)
-                for j in range(npt):
-                    v = None
-                    for c in range(nx):
-                        h = hf_a[c, :, t].reshape(tok, ew)
-                        p = jnp.dot(h, wt[slot, c, pl.ds(j * ew, ew)], preferred_element_type=jnp.float32)
-                        v = p if v is None else v + p
-                    cols = pl.ds(pl.multiple_of((i * npt + j) * tw, 128), tw)
-                    acc[:, t, :, cols] = v.reshape(SUB, sub, tw)
-                return 0
-
-            lax.fori_loop(b0, b1, rows, 0)
+            for j in range(npt):
+                v = None
+                for p in range(nx):
+                    h = hf_a[p, some].reshape(batch * nx * sub, ew)
+                    w = jnp.dot(h, wt[slot, p, pl.ds(j * ew, ew)], preferred_element_type=jnp.float32)
+                    v = w if v is None else v + w
+                cols = pl.ds(pl.multiple_of((i * npt + j) * tw, 128), tw)
+                acc[some, :, :, cols] = v.reshape(batch, nx, sub, tw)
             return 0
 
         lax.fori_loop(0, steps, step, 0)
@@ -429,9 +502,9 @@
     def late_start():
         for c in z_sends:
             c.wait_send()
-        for c in range(nx):
+        for p in range(nx):
             for j in range(kept):
-                rows_of(c, ew + j * tok, tok, lambda ref, at: pltpu.make_async_copy(ref.at[at], z.at[c, j], ls.at[4]).start())
+                rows_of(ring(cx, p, nx), ew + j * tok, tok, lambda ref, at: pltpu.make_async_copy(ref.at[at], z.at[p, j], ls.at[4]).start())
 
     def late_wait():
         ref = z.at[:, pl.ds(0, kept)]
@@ -473,115 +546,188 @@
         for j in range(2, 6):
             got(ya.at[s, 0], sem("y", 6 * s + j))
         for c in range(ny):
-            rows, at = pl.ds(c * piece, piece), pl.ds(c * sub + s * piece, piece)
+            rows, at = pl.ds(c * piece, piece), pl.ds(c * (tok // ny) + s * piece, piece)
             total = acc[s, cx, rows] + (yb[s, 0, rows] + yb[s, 1, rows])
             ov[at, :] = (xv[at, :].astype(jnp.float32) + total).astype(ov.dtype)
 
     n0, n1, n2, n3, n4, n5, n6, n7 = range(8)
+    yes = True
+    w_issue(n1)
     zy_forward_own()
     zx_forward()
-    w_issue(n1)
     w_issue(n2)
     w_issue(n3)
-    w_issue(n4)
     w_forward(n0)
     zy_forward(n2)
-    zx_last()
-    zy_send(n3)
+    zy_last(n0)
     w_forward(n1)
-    w_forward(n2)
-    zy_last(n0)
+    got(wo_hbm, sem("wout"))
     w_ready(n1)
     up(n0, n1, n2, n0, n1)
+    zx_last()
+    w_issue(n4)
+    zy_send(n3)
     w_ready(n0)
     up(n0, n0, n1, n0, n1)
+    zy_forward(n1)
+    w_forward(n2)
     zy_last(n2)
+    w_issue(n5)
     w_ready(n2)
-    up(n0, n2, n3, n0, n1)
-    zy_forward(n1)
     up(n0, n0, n3, n2, n3)
+    zy_forward(n3)
     w_forward(n3)
-    zy_forward(n3)
     zy_last(n1)
     w_ready(n3)
     up(n0, n3, n4, n0, n3)
+    up_load(n0, n3)
     h1_a(n2)
+    up(n0, n0, n3, n1, n2, yes)
+    up_load(n2, n3)
+    h1_a(n1)
+    h1_wait(n2)
+    own_a(n2)
+    zy_last(n3)
+    up(n0, n2, n3, n0, n1, yes)
+    up_load(n0, n4)
     h1_a(n0)
-    zy_last(n3)
-    up(n0, n0, n4, n3, n4)
-    h2_a(n2)
+    up(n0, n0, n4, n3, n4, yes)
+    h1_wait(n1)
+    h2_a(n1, n0)
     h1_a(n3)
-    h2_a(n0)
-    up(n0, n0, n3, n1, n2)
-    h1_a(n1)
-    h2_a(n3)
-    h2_a(n1)
+    own_a(n1)
+    h1_wait(n0)
+    own_a(n0)
+    h2_a(n2, n0)
+    h2_a(n0, n0)
+    h1_wait(n3)
+    h2_a(n3, n0)
+    h2_a(n2, n1)
+    h2_a(n2, n2)
+    own_a_forward(n2)
+    w_forward(n4)
+    h2_a(n3, n1)
+    own_a(n3)
+    h2_a(n3, n2)
+    own_a_forward(n1)
+    h2_a(n0, n1)
+    w_forward(n5)
+    own_a_forward(n0)
+    h2_a(n1, n1)
+    h2_a(n1, n2)
+    ag_a(n0)
+    h2_a(n0, n2)
+    w_ready(n5)
+    up(n1, n5, n6, n0, n4)
+    w_issue(n6)
+    own_a_forward(n3)
     ag_a(n1)
-    w_issue(n5)
-    ag_a(n0)
-    w_forward(n4)
+    ag_a(n2)
     w_ready(n4)
     up(n1, n4, n5, n0, n4)
-    w_issue(n6)
-    ag_a(n3)
+    own_a_last(n3)
+    ag_a_forward(n0)
     ag_a_forward(n1)
-    w_forward(n5)
-    ag_a_forward(n3)
-    w_ready(n5)
-    up(n1, n5, n6, n0, n4)
-    ag_a(n2)
-    w_forward(n6)
-    ag_a_last(n3)
-    ag_a_forward(n0)
-    got(wo_hbm, sem("wout"))
-    down_early(n3, n4)
+    own_a_last(n1)
+    w_forward_near(n6)
+    h2_a(n3, n3)
+    up_near(n6)
+    own_a_last(n0)
+    w_forward_far(n6)
+    ag_a_last(n0)
     ag_a_forward(n2)
-    w_ready(n6)
-    up(n1, n6, n7, n0, n4)
+    up_far(n6)
+    down_early_load()
     h1_b(n0)
     h1_b(n1)
-    ag_a_last(n0)
-    down_early(n0, n1)
+    h1_b(n2)
+    h1_b(n3)
+    own_a_last(n2)
+    h2_a(n0, n3)
+    h1_b(n4)
+    ag_a_last(n2)
     h2_b(n0)
+    h1_b(n5)
+    down_early(n0, yes)
+    down_early_load()
+    ag_b(n0)
+    h2_b(n1)
+    h2_b(n2)
+    h2_b(n3)
+    h1_b(n6)
+    h2_a(n1, n3)
+    ag_b(n1)
+    h2_b(n4)
+    h2_b(n5)
+    ag_b_forward(n0)
     ag_a_last(n1)
-    ag_a_last(n2)
-    h1_b(n2)
     late_start()
-    h2_b(n1)
-    ag_b(n0)
-    down_early(n2, n3)
-    h1_b(n3)
-    h2_b(n2)
-    ag_b_forward(n0)
-    down_early(n1, n2)
+    h2_a(n2, n3)
+    ag_b(n2)
+    down_early(n1, yes)
+    down_early_load()
+    ag_b_forward(n1)
+    h2_b(n6)
+    ag_b(n3)
+    ag_b_last(n0)
+    h1_b(n7)
     late_wait()
-    h2_b(n3)
-    ag_b(n1)
-    ag_b_last(n0)
     down_late(n0)
     y_send(n0)
-    ag_b_forward(n1)
-    y_forward(n0)
-    ag_b(n2)
+    ag_b_forward(n2)
+    ag_b(n4)
     ag_b_last(n1)
     down_late(n1)
     y_send(n1)
-    ag_b_forward(n2)
-    y_forward(n1)
+    y_forward(n0)
+    down_early(n2, yes)
+    down_early_load()
     ag_b_last(n2)
-    ag_b(n3)
+    ag_b(n5)
+    h2_b(n7)
     down_late(n2)
     y_send(n2)
-    y_final(n0)
     ag_b_forward(n3)
+    ag_b_forward(n4)
+    ag_b_forward(n5)
     y_forward(n2)
+    ag_a(n3)
     ag_b_last(n3)
     down_late(n3)
     y_send(n3)
+    ag_b(n6)
+    ag_b_last(n4)
+    ag_b_last(n5)
+    down_late(n4)
+    y_send(n4)
+    y_final(n2)
+    down_late(n5)
+    y_send(n5)
+    y_forward(n1)
+    ag_a_forward(n3)
+    y_forward(n5)
+    y_forward(n4)
+    ag_b_forward(n6)
+    y_forward(n3)
+    ag_b(n7)
+    ag_a_last(n3)
+    down_early(n3, yes)
+    ag_b_last(n6)
+    down_late(n6)
+    y_send(n6)
+    ag_b_forward(n7)
+    y_final(n5)
     y_final(n1)
-    y_final(n2)
-    y_forward(n3)
+    y_forward(n6)
+    ag_b_last(n7)
+    down_late(n7)
+    y_send(n7)
+    y_final(n6)
     y_final(n3)
+    y_final(n0)
+    y_final(n4)
+    y_forward(n7)
+    y_final(n7)
     out = pltpu.make_async_copy(ov, y_hbm, ls.at[0])
     out.start()
     for c in sends:
@@ -635,6 +781,7 @@
                 pltpu.VMEM((nx, SUB, nx, ny, piece, ew), bf),
                 pltpu.VMEM((nx, SUB, nx, ny, piece, lw), bf),
                 pltpu.VMEM((SUB, nx, sub, dloc), f32),
+                pltpu.VMEM((nx, tok, tw), f32),
                 pltpu.VMEM((SUB, 2, sub // 2, dloc), f32),
                 pltpu.VMEM((SUB, 2, sub, dloc), f32),
                 pltpu.VMEM((tok, dloc), bf),

time: 353 us -> 336 us (0.952)
  Pallas kernels: 348 us -> 334 us
    pallas_call x1, Pallas kernels: 348 us -> 334 us  [local_block(): pl.pallas_call(functools.partial(block, (nx, ny, dloc * ny)), name='mlp_b...]
where the time goes in v3:
time: 336 us
  Pallas kernels  334 us (99%)
    pallas_call x1, Pallas kernels, local_block(): pl.pallas_call(functools.partial(block, (nx, ny, dloc * ny)), name='mlp_b...  334 us

profile of v3, /device:TPU:96, one launch (start us, length us, event | category | flops | bytes accessed | tf_op | source)
XLA Modules:
  0.0 336.1 jit_solution(4357287396647479396)
XLA Ops:
  0.0 333.8 %mlp_block.1 = (bf16[256,2048]{1,0:T(8,128)(2,1)}, bf16[7,8,1024,256]{3,2,1,0:T(8,128)(2,1)}, bf16[3584,2048]{1,0:T(8,128)(2,1)}, bf16[4,8,4,8,1024]{4,3,2,1,0:T(8,128)(2,1)}, bf16[4,8,4,8,768]{4,3,2,1,0:T(8,128)(2,1)}) custom-call(bf16[256,2048]{1,0:T(8,128)(2,1)} %x_hbm.1, f32[1,2048]{1,0:T(1,128)} %bitcast.1, bf16[1024,7168]{1,0:T(8,128)(2,1)} %win.1, ...), custom_call_target="tpu_custom_call" | custom-call | tf_op jit(solution)/shard_map/mlp_block/pallas_call | solution.py:754
  333.8 2.3 copy.6

commit v4 on v3

v4 whole, which is shorter than its diff:
```python
import functools

import jax
import jax.numpy as jnp
from jax import lax
from jax.experimental import pallas as pl
from jax.experimental.pallas import tpu as pltpu
from jax.sharding import PartitionSpec as P

NORM_EPS = 1e-5
MESH = pl.DeviceIdType.MESH
NEAR_FIRST = (1, 3, 2)
SUB = 8
GROUPS = 4
LATE = 3


def gelu(v):
    return 0.5 * v * (1.0 + jnp.tanh(0.7978845608028654 * (v + 0.044715 * (v * v * v))))


KINDS = (
    "stat", "gain", "mean", "raw", "zf", "zy", "w", "pair", "wout", "h1a", "h2a", "h1b", "h2b", "own", "aga", "agb", "y",
)


class Sems:
    def __init__(self):
        self.base, self.total = {}, 0

    def add(self, name, count):
        self.base[name] = self.total
        self.total += count

    def __call__(self, name, index=0):
        return self.base[name] + index


def plan(tiles):
    s = Sems()
    for name, count in (
        ("stat", 1), ("gain", 1), ("mean", 2), ("zx", 4), ("zy", 16), ("rest", 4), ("w", 3 * tiles), ("wf", tiles + 1),
        ("wout", 1), ("h1a", 4), ("h1b", SUB), ("h2a", GROUPS), ("h2b", SUB),
        ("own", 12), ("aga", 3 * GROUPS), ("agb", 3 * SUB), ("y", 3 * SUB),
    ):
        s.add(name, count)
    return s


def block(n, x_hbm, gain_ref, win, wout, ov, w_hbm, wo_hbm, hst_a, hst_b,
          xv, sums, stat, means, gains, z, wt, hm_a, hm_b, hf_a, hf_b, acc, pre, ya, yb, ss, rs, ls):
    nx, ny, d_model = n
    row, cy = lax.axis_index("row"), lax.axis_index("col")
    cx, k = row // 2, lax.rem(row, 2)
    tok, dloc = ov.shape
    tiles, krows, tw = w_hbm.shape[0], w_hbm.shape[2], w_hbm.shape[3]
    early = tiles - LATE
    half = tok // 2
    sub = tok // SUB
    piece = sub // ny
    batch = SUB // GROUPS
    sem = plan(tiles)

    def ring(v, d, m):
        return lax.rem(v + (d + m), m)

    def dev(dx=0, dy=0, core=None):
        return {"row": 2 * ring(cx, dx, nx) + (k if core is None else core), "col": ring(cy, dy, ny)}

    partner = dev(core=1 - k)

    def remote(src, dst, where, i, kind):
        return pltpu.make_async_remote_copy(
            src_ref=src, dst_ref=dst, send_sem=ss.at[KINDS.index(kind)], recv_sem=rs.at[i], device_id=where, device_id_type=MESH
        )

    def send(src, dst, where, i, kind):
        remote(src, dst, where, i, kind).start()

    def got(ref, i):
        remote(ref, ref, partner, i, "w").wait_recv()

    def drain(kind, ref):
        remote(ref, ref, partner, 0, kind).wait_send()

    barrier = pltpu.get_barrier_semaphore()
    peers = [partner] + [dev(dx=d) for d in range(1, nx)] + [dev(dy=d) for d in range(1, ny)]
    for p in peers:
        pl.semaphore_signal(barrier, inc=1, device_id=p, device_id_type=MESH)
    load_x = pltpu.make_async_copy(x_hbm, xv, ls.at[0])
    load_x.start()
    pl.semaphore_wait(barrier, len(peers))

    off = (0, 1, 3, 2)
    lo, hi = pl.ds(0, half), pl.ds(half, half)

    def zb(b, dy, rows=None):
        ref = z.at[ring(cx, off[b], nx), ring(cy, dy, ny)]
        return ref if rows is None else ref.at[rows]

    def raw(rows, where, i):
        send(x_hbm.at[rows], zb(0, 0, rows), where, i, "raw")

    raw(lo, dev(dy=1), sem("zy", 0))
    raw(hi, dev(dy=-1), sem("zy", 1))
    raw(lo, dev(dx=1), sem("zx", 0))
    raw(hi, dev(dx=-1), sem("zx", 1))
    load_x.wait()

    lane = lax.broadcasted_iota(jnp.int32, (32, sums.shape[2]), 1)

    def part(i, _):
        at = pl.ds(pl.multiple_of(i * 32, 32), 32)
        v = xv[at, :].astype(jnp.float32)
        s1 = jnp.sum(v, axis=1, keepdims=True)
        s2 = jnp.sum(v * v, axis=1, keepdims=True)
        sums[0, at, :] = jnp.where(lane == 0, s1, s2)
        return 0

    lax.fori_loop(0, tok // 32, part, 0)
    stat[cy] = jnp.transpose(sums[0])[: stat.shape[1]]
    gains[cy] = gain_ref[...]
    for d in NEAR_FIRST:
        send(stat.at[cy], stat.at[cy], dev(dy=d), sem("stat"), "stat")
    for d in NEAR_FIRST:
        send(gains.at[cy], gains.at[cy], dev(dy=d), sem("gain"), "gain")
    raw(hi, dev(dy=1), sem("rest", 0))
    raw(lo, dev(dy=-1), sem("rest", 1))
    raw(hi, dev(dx=1), sem("rest", 2))
    raw(lo, dev(dx=-1), sem("rest", 3))

    def columns(dx, t):
        return pl.ds(pl.multiple_of(ring(cx, dx, nx) * (tiles * tw) + t * tw, 128), tw)

    last = tiles - 1

    def w_issue(t):
        for d in NEAR_FIRST:
            send(win.at[:, columns(d, t)], w_hbm.at[t, row], dev(dx=d), sem("w", 3 * t + d - 1), "w")
        send(win.at[:, columns(0, t)], w_hbm.at[t, row], partner, sem("wf", t), "pair")

    def w_pass(t, ds):
        for d in ds:
            slot = 2 * ring(cx, -d, nx) + k
            got(w_hbm.at[t, slot], sem("w", 3 * t + d - 1))
            i = sem("wf", tiles if t == last and d == NEAR_FIRST[-1] else t)
            send(w_hbm.at[t, slot], w_hbm.at[t, slot], partner, i, "pair")

    def w_forward(t):
        w_pass(t, NEAR_FIRST)

    def w_ready(t):
        got(w_hbm.at[t, pl.ds(0, nx)], sem("wf", t))

    def w_forward_near(t):
        w_pass(t, NEAR_FIRST[:-1])

    def w_forward_far(t):
        w_pass(t, NEAR_FIRST[-1:])

    got(stat.at[pl.ds(0, ny - 1)], sem("stat"))
    total = (stat[0] + stat[1]) + (stat[2] + stat[3])
    mean = total[0:1] / d_model
    rstd = lax.rsqrt(total[1:2] / d_model - mean * mean + NORM_EPS)
    means[0] = jnp.where(lax.broadcasted_iota(jnp.int32, total.shape, 0) == 0, mean, rstd)
    send(means.at[0], means.at[2], dev(dx=1), sem("mean", 0), "mean")
    send(means.at[0], means.at[1], dev(dx=-1), sem("mean", 1), "mean")
    w_issue(0)
    send(wout, wo_hbm, partner, sem("wout"), "wout")

    def spread(b):
        copies = sums.shape[2] // means.shape[1]
        sums[b] = jnp.transpose(jnp.concatenate([means[b]] * copies, axis=0))

    def normalise(b, y, src=None, r0=0, r1=tok):
        t = ring(cx, off[b], nx)

        def norm(i, _):
            at = pl.ds(pl.multiple_of(i * 32, 32), 32)
            v = (z[t, y, at, :] if src is None else src[at, :]).astype(jnp.float32)
            z[t, y, at, :] = ((v - sums[b, at, 0:1]) * sums[b, at, 1:2] * gains[y]).astype(z.dtype)
            return 0

        lax.fori_loop(r0 // 32, r1 // 32, norm, 0)

    spread(0)
    normalise(0, cy, xv)

    up_y, down_y, far_y = ring(cy, 1, ny), ring(cy, -1, ny), ring(cy, 2, ny)

    def zx_forward():
        got(zb(2, 0, lo), sem("zx", 0))
        got(means.at[0], sem("mean", 0))
        got(zb(2, 0, hi), sem("rest", 2))
        spread(2)
        normalise(2, cy)
        send(zb(2, 0, lo), zb(2, 0, lo), dev(dx=1), sem("zx", 2), "zf")
        zy_send(2)
        got(zb(1, 0, hi), sem("zx", 1))
        got(means.at[0], sem("mean", 1))
        got(zb(1, 0, lo), sem("rest", 3))
        spread(1)
        normalise(1, cy)
        send(zb(1, 0, hi), zb(1, 0, hi), dev(dx=-1), sem("zx", 3), "zf")
        zy_send(1)

    def zx_last():
        got(zb(3, 0, lo), sem("zx", 2))
        got(zb(3, 0, hi), sem("zx", 3))

    def zy_send(b):
        send(zb(b, 0), zb(b, 0), dev(dy=1), sem("zy", 4 * b), "zy")
        send(zb(b, 0), zb(b, 0), dev(dy=-1), sem("zy", 4 * b + 1), "zy")

    def zy_forward(b):
        got(zb(b, -1), sem("zy", 4 * b))
        send(zb(b, -1, lo), zb(b, -1, lo), dev(dy=1), sem("zy", 4 * b + 2), "zy")
        got(zb(b, 1), sem("zy", 4 * b + 1))
        send(zb(b, 1, hi), zb(b, 1, hi), dev(dy=-1), sem("zy", 4 * b + 3), "zy")

    def zy_last(b):
        got(zb(b, 2, lo), sem("zy", 4 * b + 2))
        got(zb(b, 2, hi), sem("zy", 4 * b + 3))

    def zy_own_near():
        got(gains.at[pl.ds(0, ny - 1)], sem("gain"))
        got(zb(0, -1, lo), sem("zy", 0))
        normalise(0, down_y, None, 0, half)
        send(zb(0, -1, lo), zb(0, -1, lo), dev(dy=1), sem("zy", 2), "zf")
        got(zb(0, 1, hi), sem("zy", 1))
        normalise(0, up_y, None, half, tok)
        send(zb(0, 1, hi), zb(0, 1, hi), dev(dy=-1), sem("zy", 3), "zf")

    def zy_own_rest():
        got(zb(0, -1, hi), sem("rest", 0))
        normalise(0, down_y, None, half, tok)
        got(zb(0, 1, lo), sem("rest", 1))
        normalise(0, up_y, None, 0, half)

    def wt_rows(t, slot, rows):
        for j in rows:
            for core in range(2):
                r = 2 * ring(cx, j, nx) + lax.rem(k + core, 2)
                dst = wt.at[slot, r // 2, pl.ds(pl.multiple_of(lax.rem(r, 2) * krows, krows), krows)]
                src = win.at[:, columns(0, t)] if j == 0 and core == 0 else w_hbm.at[t, r]
                pltpu.make_async_copy(src, dst, ls.at[1 + slot]).start()

    def wt_load(t, slot):
        wt_rows(t, slot, range(nx))

    def wt_wait(slot):
        pltpu.make_async_copy(wt.at[slot], wt.at[slot], ls.at[1 + slot]).wait()

    def up_load(t0, t1):
        for i in range(min(2, t1 - t0)):
            wt_load(t0 + i, i)

    def up(late, t0, t1, b0, b1, loaded=False):
        hm, hf, first = (hm_b, hf_b, early) if late else (hm_a, hf_a, 0)
        if not loaded:
            up_load(t0, t1)

        def tile(i, _):
            slot = lax.rem(i, 3)
            wt_wait(slot)

            @pl.when(i + 2 < t1 - t0)
            def _():
                wt_load(t0 + i + 2, lax.rem(i + 2, 3))

            at = pl.ds(pl.multiple_of((t0 + i - first) * tw, 128), tw)

            def rows(b, _):
                t = ring(cx, b + b // 2 - 2 * (b // 3), nx)
                v = jnp.dot(z[t, 0], wt[slot, 0], preferred_element_type=jnp.float32)
                for j in range(1, ny):
                    v += jnp.dot(z[t, j], wt[slot, j], preferred_element_type=jnp.float32)
                hm[t, :, :, :, at] = gelu(v).astype(hm.dtype).reshape(ny, SUB, piece, tw)

                @pl.when(cx == cy)
                def _():
                    hf[0, :, t, cy, :, at] = hm[t, cy, :, :, at]

                return 0

            lax.fori_loop(b0, b1, rows, 0)
            return 0

        lax.fori_loop(0, t1 - t0, tile, 0)

    def up_near(t):
        got(w_hbm.at[t, pl.ds(0, nx - 1)], sem("wf", t))
        wt_rows(t, 0, (0, 1, 3))
        ref = wt.at[0, pl.ds(0, ny - 1)]
        pltpu.make_async_copy(ref, ref, ls.at[1]).wait()

        def rows(b, _):
            v = None
            for j in (0, 1, 3):
                f = ring(cx, j, nx)
                p = jnp.dot(z[b, f], wt[0, f], preferred_element_type=jnp.float32)
                v = p if v is None else v + p
            pre[b] = v
            return 0

        lax.fori_loop(0, nx, rows, 0)

    def up_far(t):
        got(w_hbm.at[t, row], sem("wf", tiles))
        wt_rows(t, 0, (2,))
        f = ring(cx, 2, nx)
        pltpu.make_async_copy(wt.at[0, f], wt.at[0, f], ls.at[1]).wait()
        at = pl.ds((t - early) * tw, tw)

        def rows(b, _):
            v = pre[b] + jnp.dot(z[b, f], wt[0, f], preferred_element_type=jnp.float32)
            hm_b[b, :, :, :, at] = gelu(v).astype(hm_b.dtype).reshape(ny, SUB, piece, tw)

            @pl.when(cx == cy)
            def _():
                hf_b[0, :, b, cy, :, at] = hm_b[b, cy, :, :, at]

            return 0

        lax.fori_loop(0, nx, rows, 0)

    def h1_a(b):
        t = ring(cx, off[b], nx)
        for d in NEAR_FIRST:
            c = ring(cy, d, ny)
            i = sem("h1a", b)

            @pl.when(cx == cy)
            def _():
                remote(hm_a.at[t, c], hf_a.at[0, :, t, c], dev(dy=d), i, "h1a").start()

            @pl.when(cx != cy)
            def _():
                remote(hm_a.at[t, c], hst_a.at[cy, :, t], dev(dy=d), i, "h1a").start()

    def h1_wait(b):
        got(hst_a.at[pl.ds(0, ny - 1), :, 0], sem("h1a", b))

    def h2_a(b, g):
        t = ring(cx, off[b], nx)
        some = pl.ds(g * batch, batch)
        for d in NEAR_FIRST:
            c = ring(cx, d, nx)
            i = sem("h2a", g)

            @pl.when(c == cy)
            def _():
                remote(hm_a.at[t, cy, some], hf_a.at[nx - d, some, t, cy], dev(dx=d), i, "h2a").start()

            @pl.when(c != cy)
            def _():
                remote(hst_a.at[c, some, t], hf_a.at[nx - d, some, t, cy], dev(dx=d), i, "h2a").start()

    def h1_b(s):
        for d in NEAR_FIRST:
            c = ring(cy, d, ny)
            i = sem("h1b", s)

            @pl.when(cx == cy)
            def _():
                remote(hm_b.at[:, c, s], hf_b.at[0, s, :, c], dev(dy=d), i, "h1b").start()

            @pl.when(cx != cy)
            def _():
                remote(hm_b.at[:, c, s], hst_b.at[cy, s], dev(dy=d), i, "h1b").start()

    def h2_b(s):
        got(hst_b.at[pl.ds(0, ny - 1), 0], sem("h1b", s))
        for d in NEAR_FIRST:
            c = ring(cx, d, nx)
            i = sem("h2b", s)

            @pl.when(c == cy)
            def _():
                remote(hm_b.at[:, cy, s], hf_b.at[nx - d, s, :, cy], dev(dx=d), i, "h2b").start()

            @pl.when(c != cy)
            def _():
                remote(hst_b.at[c, s], hf_b.at[nx - d, s, :, cy], dev(dx=d), i, "h2b").start()

    def gather(kind, i, whole, low, high):
        def begin():
            send(whole(cy), whole(cy), dev(dy=1), i, kind)
            send(whole(cy), whole(cy), dev(dy=-1), i + 1, kind)

        def forward():
            got(whole(cy), i)
            send(low(down_y), low(down_y), dev(dy=1), i + 2, kind)
            got(whole(cy), i + 1)
            send(high(up_y), high(up_y), dev(dy=-1), i + 2, kind)

        def last():
            got(whole(far_y), i + 2)

        return begin, forward, last

    def gather_own(b):
        t = ring(cx, off[b], nx)
        part = lambda s, n: lambda y: hf_a.at[0, pl.ds(s, n), t, y]
        return gather("own", sem("own", 3 * b), part(0, SUB), part(0, SUB // 2), part(SUB // 2, SUB // 2))

    def gather_a(g):
        part = lambda s, n: lambda y: hf_a.at[pl.ds(1, nx - 1), pl.ds(g * batch + s, n), :, y]
        return gather("aga", sem("aga", 3 * g), part(0, batch), part(0, batch // 2), part(batch // 2, batch // 2))

    def gather_b(s):
        part = lambda c, n: lambda y: hf_b.at[pl.ds(c, n), s, :, y]
        return gather("agb", sem("agb", 3 * s), part(0, nx), part(0, nx // 2), part(nx // 2, nx // 2))

    own_gathers = [gather_own(b) for b in range(nx)]
    a_gathers = [gather_a(g) for g in range(GROUPS)]
    b_gathers = [gather_b(s) for s in range(SUB)]

    def own_a(b):
        own_gathers[b][0]()

    def own_a_forward(b):
        own_gathers[b][1]()

    def own_a_last(b):
        own_gathers[b][2]()

    def ag_a(g):
        got(hst_a.at[pl.ds(0, nx - 1), pl.ds(0, batch)], sem("h2a", g))
        a_gathers[g][0]()

    def ag_a_forward(g):
        a_gathers[g][1]()

    def ag_a_last(g):
        a_gathers[g][2]()

    def ag_b(s):
        got(hst_b.at[pl.ds(0, nx - 1), 0], sem("h2b", s))
        b_gathers[s][0]()

    def ag_b_forward(s):
        b_gathers[s][1]()

    def ag_b_last(s):
        b_gathers[s][2]()

    ew, lw = early * tw, LATE * tw
    npt = 2 * krows // ew
    steps = dloc // (npt * tw)
    kept = lw // tok

    def rows_of(c, skip, count, use):
        at = pl.ds(pl.multiple_of(lax.rem(c, 2) * (ew + lw) + skip, 128), count)

        @pl.when(c // 2 == k)
        def _():
            use(wout, at)

        @pl.when(c // 2 != k)
        def _():
            use(wo_hbm, at)

    def we_load(i, slot):
        for j in range(npt):
            for p in range(nx):
                cols = pl.ds(pl.multiple_of((i * npt + j) * tw, 128), tw)
                dst = wt.at[slot, p, pl.ds(j * ew, ew)]
                rows_of(ring(cx, p, nx), 0, ew, lambda ref, at: pltpu.make_async_copy(ref.at[at, cols], dst, ls.at[1 + slot]).start())

    def we_wait(slot):
        ref = wt.at[slot, :, pl.ds(0, npt * ew)]
        pltpu.make_async_copy(ref, ref, ls.at[1 + slot]).wait()

    def down_early_load():
        for i in range(min(2, steps)):
            we_load(i, i)

    def down_early(g, loaded=False):
        some = pl.ds(g * batch, batch)
        if not loaded:
            down_early_load()

        def step(i, _):
            slot = lax.rem(i, 3)
            we_wait(slot)

            @pl.when(i + 2 < steps)
            def _():
                we_load(i + 2, lax.rem(i + 2, 3))

            for j in range(npt):
                v = None
                for p in range(nx):
                    h = hf_a[p, some].reshape(batch * nx * sub, ew)
                    w = jnp.dot(h, wt[slot, p, pl.ds(j * ew, ew)], preferred_element_type=jnp.float32)
                    v = w if v is None else v + w
                cols = pl.ds(pl.multiple_of((i * npt + j) * tw, 128), tw)
                acc[some, :, :, cols] = v.reshape(batch, nx, sub, tw)
            return 0

        lax.fori_loop(0, steps, step, 0)

    def late_start():
        drain("zf", z.at[0, pl.ds(0, 2)])
        drain("zy", z.at[pl.ds(0, nx - 1), pl.ds(0, ny - 1)])
        for p in range(nx):
            for j in range(kept):
                rows_of(ring(cx, p, nx), ew + j * tok, tok, lambda ref, at: pltpu.make_async_copy(ref.at[at], z.at[p, j], ls.at[4]).start())

    def late_wait():
        ref = z.at[:, pl.ds(0, kept)]
        pltpu.make_async_copy(ref, ref, ls.at[4]).wait()

    def down_late(s):
        wide = 2 * tw

        def step(i, _):
            cols = pl.ds(pl.multiple_of(i * wide, 128), wide)
            v = None
            for c in range(nx):
                h = hf_b[c, s].reshape(nx * sub, lw)
                p = jnp.dot(h, z[c, pl.ds(0, kept), :, cols].reshape(lw, wide), preferred_element_type=jnp.float32)
                v = p if v is None else v + p
            acc[s, :, :, cols] += v.reshape(nx, sub, wide)
            return 0

        lax.fori_loop(0, dloc // wide, step, 0)

    top, low = pl.ds(0, sub // 2), pl.ds(sub // 2, sub // 2)
    right, left, across = ring(cx, 1, nx), ring(cx, -1, nx), ring(cx, 2, nx)

    def y_send(s):
        send(acc.at[s, across, top], ya.at[s, 0], dev(dx=1), sem("y", 3 * s), "y")
        send(acc.at[s, across, low], ya.at[s, 1], dev(dx=-1), sem("y", 3 * s + 1), "y")
        send(acc.at[s, right, low], yb.at[s, 0, low], dev(dx=1), sem("y", 3 * s + 2), "y")
        send(acc.at[s, left, top], yb.at[s, 1, top], dev(dx=-1), sem("y", 3 * s + 2), "y")

    def y_forward(s):
        got(ya.at[s, 0], sem("y", 3 * s))
        acc[s, right, top] += ya[s, 0]
        send(acc.at[s, right, top], yb.at[s, 0, top], dev(dx=1), sem("y", 3 * s + 2), "y")
        got(ya.at[s, 1], sem("y", 3 * s + 1))
        acc[s, left, low] += ya[s, 1]
        send(acc.at[s, left, low], yb.at[s, 1, low], dev(dx=-1), sem("y", 3 * s + 2), "y")

    def y_final(s):
        got(yb.at[s], sem("y", 3 * s + 2))
        for c in range(ny):
            rows, at = pl.ds(c * piece, piece), pl.ds(c * (tok // ny) + s * piece, piece)
            total = acc[s, cx, rows] + (yb[s, 0, rows] + yb[s, 1, rows])
            ov[at, :] = (xv[at, :].astype(jnp.float32) + total).astype(ov.dtype)

    n0, n1, n2, n3, n4, n5, n6, n7 = range(8)
    yes = True
    zy_own_near()
    zx_forward()
    w_issue(n1)
    w_issue(n2)
    zy_forward(n2)
    zx_last()
    zy_send(n3)
    w_issue(n3)
    w_issue(n4)
    zy_last(n0)
    w_forward(n0)
    w_forward(n1)
    zy_own_rest()
    w_ready(n1)
    up(n0, n1, n2, n0, n1)
    zy_forward(n1)
    zy_forward(n3)
    w_forward(n2)
    w_ready(n2)
    up(n0, n2, n3, n0, n1)
    zy_last(n2)
    w_forward(n3)
    zy_last(n1)
    w_ready(n0)
    up(n0, n0, n3, n2, n3)
    w_ready(n3)
    up(n0, n3, n4, n0, n3)
    up_load(n0, n4)
    h1_a(n2)
    zy_last(n3)
    up(n0, n0, n4, n3, n4, yes)
    up_load(n0, n1)
    h1_a(n3)
    h1_wait(n2)
    w_issue(n5)
    own_a(n2)
    up(n0, n0, n1, n0, n1, yes)
    up_load(n0, n3)
    h1_a(n0)
    h1_wait(n3)
    h2_a(n2, n0)
    up(n0, n0, n3, n1, n2, yes)
    h1_a(n1)
    h2_a(n3, n0)
    h1_wait(n0)
    h2_a(n0, n0)
    h2_a(n0, n1)
    own_a(n3)
    h1_wait(n1)
    own_a(n1)
    h2_a(n1, n0)
    h2_a(n2, n1)
    w_forward(n4)
    own_a(n0)
    h2_a(n2, n2)
    h2_a(n0, n2)
    own_a_forward(n2)
    own_a_forward(n3)
    own_a_forward(n1)
    own_a_last(n3)
    own_a_forward(n0)
    w_forward(n5)
    ag_a(n0)
    h2_a(n1, n1)
    h2_a(n3, n1)
    h2_a(n3, n2)
    h2_a(n1, n2)
    w_issue(n6)
    w_ready(n4)
    up(n1, n4, n5, n0, n4)
    own_a_last(n2)
    ag_a(n1)
    w_ready(n5)
    up(n1, n5, n6, n0, n4)
    ag_a(n2)
    got(wo_hbm, sem("wout"))
    ag_a_forward(n0)
    w_forward_near(n6)
    ag_a_forward(n1)
    up_near(n6)
    ag_a_forward(n2)
    w_forward_far(n6)
    up_far(n6)
    down_early_load()
    h1_b(n0)
    h1_b(n1)
    h1_b(n2)
    h1_b(n3)
    h1_b(n4)
    ag_a_last(n0)
    h1_b(n5)
    late_start()
    ag_a_last(n1)
    own_a_last(n0)
    h2_b(n0)
    own_a_last(n1)
    down_early(n0, yes)
    down_early_load()
    h2_a(n2, n3)
    h2_a(n0, n3)
    ag_b(n0)
    h2_b(n1)
    h2_a(n1, n3)
    h2_b(n2)
    h2_b(n3)
    h1_b(n6)
    h1_b(n7)
    down_early(n1, yes)
    down_early_load()
    h2_b(n4)
    ag_b_forward(n0)
    late_wait()
    ag_b(n1)
    h2_a(n3, n3)
    h2_b(n5)
    ag_b(n2)
    h2_b(n6)
    h2_b(n7)
    ag_b_last(n0)
    down_late(n0)
    y_send(n0)
    ag_b_forward(n1)
    ag_b(n3)
    ag_a_last(n2)
    down_early(n2, yes)
    down_early_load()
    ag_b_forward(n2)
    ag_b(n4)
    y_forward(n0)
    ag_b_last(n1)
    ag_b(n5)
    down_late(n1)
    y_send(n1)
    y_forward(n1)
    ag_b_last(n2)
    down_late(n2)
    ag_b_forward(n3)
    y_send(n2)
    ag_b_forward(n4)
    ag_b_forward(n5)
    ag_a(n3)
    y_forward(n2)
    ag_b_last(n3)
    down_late(n3)
    y_send(n3)
    ag_b_last(n4)
    down_late(n4)
    ag_b_last(n5)
    y_send(n4)
    y_final(n0)
    ag_b(n6)
    down_late(n5)
    ag_a_forward(n3)
    y_send(n5)
    ag_b_forward(n6)
    y_forward(n4)
    ag_b(n7)
    y_forward(n5)
    y_forward(n3)
    ag_a_last(n3)
    down_early(n3, yes)
    ag_b_last(n6)
    down_late(n6)
    y_send(n6)
    ag_b_forward(n7)
    y_final(n2)
    y_final(n1)
    y_forward(n6)
    ag_b_last(n7)
    down_late(n7)
    y_send(n7)
    y_final(n3)
    y_final(n4)
    y_final(n6)
    y_forward(n7)
    y_final(n5)
    y_final(n7)
    three = pl.ds(0, nx - 1)
    drain("stat", stat.at[three])
    drain("gain", gains.at[three])
    drain("mean", means.at[pl.ds(0, 2)])
    drain("raw", z.at[0])
    drain("w", w_hbm.at[:, three])
    drain("pair", w_hbm.at[:, pl.ds(0, nx)])
    drain("wout", wo_hbm)
    for kind in ("h1a", "h2a", "own"):
        drain(kind, hst_a.at[three])
    for kind in ("h1b", "h2b"):
        drain(kind, hst_b.at[three])
    drain("aga", hf_a.at[three, :, :, three])
    drain("agb", hf_b.at[:, :, :, three])
    drain("y", acc.at[:, three])


def solution(mesh):
    nx, ny = mesh.shape["row"] // 2, mesh.shape["col"]

    def local_block(x, gain, win, wout):
        tok, dloc = x.shape
        krows, floc = win.shape
        width = floc // nx
        tw = width // 7
        tiles = width // tw
        early = tiles - LATE
        ew, lw = early * tw, LATE * tw
        sub = tok // SUB
        piece = sub // ny
        bf, f32 = jnp.bfloat16, jnp.float32
        count = plan(tiles).total
        hbm = lambda shape, dt: jax.ShapeDtypeStruct(shape, dt)
        outs = pl.pallas_call(
            functools.partial(block, (nx, ny, dloc * ny)),
            name="mlp_block",
            out_shape=[
                pltpu.VMEM((tok, dloc), bf),
                hbm((tiles, 2 * nx, krows, tw), bf),
                hbm(wout.shape, bf),
                hbm((ny, SUB, nx, piece, ew), bf),
                hbm((ny, SUB, nx, piece, lw), bf),
            ],
            in_specs=[
                pl.BlockSpec(memory_space=pl.ANY),
                pl.BlockSpec(memory_space=pltpu.VMEM),
                pl.BlockSpec(memory_space=pl.ANY),
                pl.BlockSpec(memory_space=pl.ANY),
            ],
            out_specs=[pl.BlockSpec(memory_space=pltpu.VMEM)] + [pl.BlockSpec(memory_space=pl.ANY)] * 4,
            scratch_shapes=[
                pltpu.VMEM((tok, dloc), bf),
                pltpu.VMEM((3, tok, 128), f32),
                pltpu.VMEM((ny, 8, tok), f32),
                pltpu.VMEM((3, 8, tok), f32),
                pltpu.VMEM((ny, 1, dloc), f32),
                pltpu.VMEM((nx, ny, tok, dloc), bf),
                pltpu.VMEM((3, ny, 2 * krows, tw), bf),
                pltpu.VMEM((nx, ny, SUB, piece, ew), bf),
                pltpu.VMEM((nx, ny, SUB, piece, lw), bf),
                pltpu.VMEM((nx, SUB, nx, ny, piece, ew), bf),
                pltpu.VMEM((nx, SUB, nx, ny, piece, lw), bf),
                pltpu.VMEM((SUB, nx, sub, dloc), f32),
                pltpu.VMEM((nx, tok, tw), f32),
                pltpu.VMEM((SUB, 2, sub // 2, dloc), f32),
                pltpu.VMEM((SUB, 2, sub, dloc), f32),
                pltpu.SemaphoreType.DMA((len(KINDS),)),
                pltpu.SemaphoreType.DMA((count,)),
                pltpu.SemaphoreType.DMA((5,)),
            ],
            compiler_params=pltpu.CompilerParams(
                collective_id=0, has_side_effects=True, vmem_limit_bytes=65900000
            ),
        )(x, gain.reshape(1, dloc), win, wout)
        return outs[0]

    return jax.shard_map(
        local_block,
        mesh=mesh,
        in_specs=(P(("dp", "row"), "col"), P("col"), P("row", "col"), P("row", "col")),
        out_specs=P(("dp", "row"), "col"),
        check_vma=False,
    )
```

time: 336 us -> 327 us (0.973)
  Pallas kernels: 334 us -> 326 us
    pallas_call x1, Pallas kernels: 334 us -> 326 us  [local_block(): pl.pallas_call(functools.partial(block, (nx, ny, dloc * ny)), name='mlp_b...]
where the time goes in v4:
time: 327 us
  Pallas kernels  326 us (100%)
    pallas_call x1, Pallas kernels, local_block(): pl.pallas_call(functools.partial(block, (nx, ny, dloc * ny)), name='mlp_b...  326 us

profile of v4, /device:TPU:96, one launch (start us, length us, event | category | flops | bytes accessed | tf_op | source)
XLA Modules:
  0.0 326.7 jit_solution(2403917272791155580)
XLA Ops:
  0.0 325.7 %mlp_block.1 = (bf16[256,2048]{1,0:T(8,128)(2,1)S(1)}, bf16[7,8,1024,256]{3,2,1,0:T(8,128)(2,1)}, bf16[3584,2048]{1,0:T(8,128)(2,1)}, bf16[4,8,4,8,1024]{4,3,2,1,0:T(8,128)(2,1)}, bf16[4,8,4,8,768]{4,3,2,1,0:T(8,128)(2,1)}) custom-call(bf16[256,2048]{1,0:T(8,128)(2,1)} %x_hbm.1, f32[1,2048]{1,0:T(1,128)} %bitcast.1, bf16[1024,7168]{1,0:T(8,128)(2,1)} %win.1, ...), custom_call_target="tpu_custom_call" | custom-call | tf_op jit(solution)/shard_map/mlp_block/pallas_call | solution.py:766
  325.7 1.0 copy.6

commit v5 on v4

--- a/solution.py
+++ b/solution.py
@@ -12,7 +12,7 @@
 NEAR_FIRST = (1, 3, 2)
 SUB = 8
 GROUPS = 4
-LATE = 3
+MID, LATE = 2, 2
 
 
 def gelu(v):
@@ -20,7 +20,7 @@
 
 
 KINDS = (
-    "stat", "gain", "mean", "raw", "zf", "zy", "w", "pair", "wout", "h1a", "h2a", "h1b", "h2b", "own", "aga", "agb", "y",
+    "stat", "gain", "mean", "raw", "zf", "zy", "w", "pair", "wout", "h1a", "h2a", "h1b", "h2b", "own", "aga", "h1m", "h2m", "agm", "agb", "y",
 )
 
 
@@ -40,21 +40,21 @@
     s = Sems()
     for name, count in (
         ("stat", 1), ("gain", 1), ("mean", 2), ("zx", 4), ("zy", 16), ("rest", 4), ("w", 3 * tiles), ("wf", tiles + 1),
-        ("wout", 1), ("h1a", 4), ("h1b", SUB), ("h2a", GROUPS), ("h2b", SUB),
-        ("own", 12), ("aga", 3 * GROUPS), ("agb", 3 * SUB), ("y", 3 * SUB),
+        ("wout", 1), ("h1a", 4), ("h1m", SUB), ("h1b", SUB), ("h2a", GROUPS), ("h2m", SUB), ("h2b", SUB),
+        ("own", 12), ("aga", 3 * GROUPS), ("agm", 3 * SUB), ("agb", 3 * SUB), ("y", 3 * SUB),
     ):
         s.add(name, count)
     return s
 
 
-def block(n, x_hbm, gain_ref, win, wout, ov, w_hbm, wo_hbm, hst_a, hst_b,
-          xv, sums, stat, means, gains, z, wt, hm_a, hm_b, hf_a, hf_b, acc, pre, ya, yb, ss, rs, ls):
+def block(n, x_hbm, gain_ref, win, wout, ov, w_hbm, wo_hbm, hst_a, hst_m, hst_b,
+          xv, sums, stat, means, gains, z, wt, hm_a, hm_m, hm_b, hf_a, hf_m, hf_b, acc, pre, ya, yb, ss, rs, ls):
     nx, ny, d_model = n
     row, cy = lax.axis_index("row"), lax.axis_index("col")
     cx, k = row // 2, lax.rem(row, 2)
     tok, dloc = ov.shape
     tiles, krows, tw = w_hbm.shape[0], w_hbm.shape[2], w_hbm.shape[3]
-    early = tiles - LATE
+    early = tiles - MID - LATE
     half = tok // 2
     sub = tok // SUB
     piece = sub // ny
@@ -255,8 +255,8 @@
         for i in range(min(2, t1 - t0)):
             wt_load(t0 + i, i)
 
-    def up(late, t0, t1, b0, b1, loaded=False):
-        hm, hf, first = (hm_b, hf_b, early) if late else (hm_a, hf_a, 0)
+    def up(part, t0, t1, b0, b1, loaded=False):
+        hm, hf, first = ((hm_a, hf_a, 0), (hm_m, hf_m, early), (hm_b, hf_b, early + MID))[part]
         if not loaded:
             up_load(t0, t1)
 
@@ -310,7 +310,7 @@
         wt_rows(t, 0, (2,))
         f = ring(cx, 2, nx)
         pltpu.make_async_copy(wt.at[0, f], wt.at[0, f], ls.at[1]).wait()
-        at = pl.ds((t - early) * tw, tw)
+        at = pl.ds((t - early - MID) * tw, tw)
 
         def rows(b, _):
             v = pre[b] + jnp.dot(z[b, f], wt[0, f], preferred_element_type=jnp.float32)
@@ -356,32 +356,38 @@
             def _():
                 remote(hst_a.at[c, some, t], hf_a.at[nx - d, some, t, cy], dev(dx=d), i, "h2a").start()
 
-    def h1_b(s):
-        for d in NEAR_FIRST:
-            c = ring(cy, d, ny)
-            i = sem("h1b", s)
-
-            @pl.when(cx == cy)
-            def _():
-                remote(hm_b.at[:, c, s], hf_b.at[0, s, :, c], dev(dy=d), i, "h1b").start()
-
-            @pl.when(cx != cy)
-            def _():
-                remote(hm_b.at[:, c, s], hst_b.at[cy, s], dev(dy=d), i, "h1b").start()
-
-    def h2_b(s):
-        got(hst_b.at[pl.ds(0, ny - 1), 0], sem("h1b", s))
-        for d in NEAR_FIRST:
-            c = ring(cx, d, nx)
-            i = sem("h2b", s)
-
-            @pl.when(c == cy)
-            def _():
-                remote(hm_b.at[:, cy, s], hf_b.at[nx - d, s, :, cy], dev(dx=d), i, "h2b").start()
-
-            @pl.when(c != cy)
-            def _():
-                remote(hst_b.at[c, s], hf_b.at[nx - d, s, :, cy], dev(dx=d), i, "h2b").start()
+    def spread_h(kind, hm, hst, hf):
+        def h1(s):
+            for d in NEAR_FIRST:
+                c = ring(cy, d, ny)
+                i = sem("h1" + kind, s)
+
+                @pl.when(cx == cy)
+                def _():
+                    remote(hm.at[:, c, s], hf.at[0, s, :, c], dev(dy=d), i, "h1" + kind).start()
+
+                @pl.when(cx != cy)
+                def _():
+                    remote(hm.at[:, c, s], hst.at[cy, s], dev(dy=d), i, "h1" + kind).start()
+
+        def h2(s):
+            got(hst.at[pl.ds(0, ny - 1), 0], sem("h1" + kind, s))
+            for d in NEAR_FIRST:
+                c = ring(cx, d, nx)
+                i = sem("h2" + kind, s)
+
+                @pl.when(c == cy)
+                def _():
+                    remote(hm.at[:, cy, s], hf.at[nx - d, s, :, cy], dev(dx=d), i, "h2" + kind).start()
+
+                @pl.when(c != cy)
+                def _():
+                    remote(hst.at[c, s], hf.at[nx - d, s, :, cy], dev(dx=d), i, "h2" + kind).start()
+
+        return h1, h2
+
+    h1_m, h2_m = spread_h("m", hm_m, hst_m, hf_m)
+    h1_b, h2_b = spread_h("b", hm_b, hst_b, hf_b)
 
     def gather(kind, i, whole, low, high):
         def begin():
@@ -408,13 +414,20 @@
         part = lambda s, n: lambda y: hf_a.at[pl.ds(1, nx - 1), pl.ds(g * batch + s, n), :, y]
         return gather("aga", sem("aga", 3 * g), part(0, batch), part(0, batch // 2), part(batch // 2, batch // 2))
 
-    def gather_b(s):
-        part = lambda c, n: lambda y: hf_b.at[pl.ds(c, n), s, :, y]
-        return gather("agb", sem("agb", 3 * s), part(0, nx), part(0, nx // 2), part(nx // 2, nx // 2))
+    def gather_late(kind, s, hst, hf):
+        part = lambda c, n: lambda y: hf.at[pl.ds(c, n), s, :, y]
+        begin, forward, last = gather("ag" + kind, sem("ag" + kind, 3 * s), part(0, nx), part(0, nx // 2), part(nx // 2, nx // 2))
+
+        def start():
+            got(hst.at[pl.ds(0, nx - 1), 0], sem("h2" + kind, s))
+            begin()
+
+        return start, forward, last
 
     own_gathers = [gather_own(b) for b in range(nx)]
     a_gathers = [gather_a(g) for g in range(GROUPS)]
-    b_gathers = [gather_b(s) for s in range(SUB)]
+    m_gathers = [gather_late("m", s, hst_m, hf_m) for s in range(SUB)]
+    b_gathers = [gather_late("b", s, hst_b, hf_b) for s in range(SUB)]
 
     def own_a(b):
         own_gathers[b][0]()
@@ -435,8 +448,16 @@
     def ag_a_last(g):
         a_gathers[g][2]()
 
+    def ag_m(s):
+        m_gathers[s][0]()
+
+    def ag_m_forward(s):
+        m_gathers[s][1]()
+
+    def ag_m_last(s):
+        m_gathers[s][2]()
+
     def ag_b(s):
-        got(hst_b.at[pl.ds(0, nx - 1), 0], sem("h2b", s))
         b_gathers[s][0]()
 
     def ag_b_forward(s):
@@ -445,13 +466,13 @@
     def ag_b_last(s):
         b_gathers[s][2]()
 
-    ew, lw = early * tw, LATE * tw
+    ew, mw, lw = early * tw, MID * tw, LATE * tw
     npt = 2 * krows // ew
     steps = dloc // (npt * tw)
-    kept = lw // tok
+    kept, kept_m = (mw + lw) // tok, mw // tok
 
     def rows_of(c, skip, count, use):
-        at = pl.ds(pl.multiple_of(lax.rem(c, 2) * (ew + lw) + skip, 128), count)
+        at = pl.ds(pl.multiple_of(lax.rem(c, 2) * (ew + mw + lw) + skip, 128), count)
 
         @pl.when(c // 2 == k)
         def _():
@@ -518,10 +539,11 @@
         def step(i, _):
             cols = pl.ds(pl.multiple_of(i * wide, 128), wide)
             v = None
-            for c in range(nx):
-                h = hf_b[c, s].reshape(nx * sub, lw)
-                p = jnp.dot(h, z[c, pl.ds(0, kept), :, cols].reshape(lw, wide), preferred_element_type=jnp.float32)
-                v = p if v is None else v + p
+            for hf, at, depth in ((hf_m, pl.ds(0, kept_m), mw), (hf_b, pl.ds(kept_m, kept - kept_m), lw)):
+                for c in range(nx):
+                    h = hf[c, s].reshape(nx * sub, depth)
+                    p = jnp.dot(h, z[c, at, :, cols].reshape(depth, wide), preferred_element_type=jnp.float32)
+                    v = p if v is None else v + p
             acc[s, :, :, cols] += v.reshape(nx, sub, wide)
             return 0
 
@@ -557,178 +579,218 @@
     zx_forward()
     w_issue(n1)
     w_issue(n2)
-    zy_forward(n2)
-    zx_last()
-    zy_send(n3)
     w_issue(n3)
     w_issue(n4)
+    w_issue(n5)
     zy_last(n0)
+    zy_own_rest()
+    zx_last()
     w_forward(n0)
+    zy_forward(n2)
+    zy_send(n3)
     w_forward(n1)
-    zy_own_rest()
     w_ready(n1)
     up(n0, n1, n2, n0, n1)
     zy_forward(n1)
+    w_forward(n2)
     zy_forward(n3)
-    w_forward(n2)
+    zy_last(n2)
+    w_ready(n0)
     w_ready(n2)
-    up(n0, n2, n3, n0, n1)
-    zy_last(n2)
+    up(n0, n0, n3, n2, n3)
+    up_load(n2, n3)
+    h1_a(n2)
+    up(n0, n2, n3, n0, n1, yes)
+    up(n0, n0, n1, n0, n1)
+    up_load(n0, n3)
+    h1_a(n0)
     w_forward(n3)
     zy_last(n1)
-    w_ready(n0)
-    up(n0, n0, n3, n2, n3)
-    w_ready(n3)
-    up(n0, n3, n4, n0, n3)
-    up_load(n0, n4)
-    h1_a(n2)
-    zy_last(n3)
-    up(n0, n0, n4, n3, n4, yes)
-    up_load(n0, n1)
-    h1_a(n3)
-    h1_wait(n2)
-    w_issue(n5)
-    own_a(n2)
-    up(n0, n0, n1, n0, n1, yes)
-    up_load(n0, n3)
-    h1_a(n0)
-    h1_wait(n3)
-    h2_a(n2, n0)
     up(n0, n0, n3, n1, n2, yes)
     h1_a(n1)
-    h2_a(n3, n0)
+    zy_last(n3)
+    w_ready(n3)
+    up(n1, n3, n4, n0, n4)
+    up_load(n0, n3)
     h1_wait(n0)
+    h1_wait(n2)
+    own_a(n0)
+    own_a(n2)
+    w_forward(n4)
+    up(n0, n0, n3, n3, n4, yes)
+    h1_wait(n1)
+    own_a(n1)
+    h1_a(n3)
+    own_a_forward(n0)
+    own_a_forward(n2)
+    w_ready(n4)
+    up(n1, n4, n5, n0, n4)
+    h1_m(n0)
+    h1_m(n1)
     h2_a(n0, n0)
     h2_a(n0, n1)
+    h2_a(n2, n0)
+    h1_m(n2)
+    h2_a(n1, n0)
+    h1_m(n3)
+    h1_m(n4)
+    h1_m(n5)
+    h1_wait(n3)
     own_a(n3)
-    h1_wait(n1)
-    own_a(n1)
-    h2_a(n1, n0)
+    h2_a(n3, n0)
+    h2_m(n0)
+    h2_a(n1, n1)
+    got(wo_hbm, sem("wout"))
+    h1_m(n6)
+    h1_m(n7)
+    w_forward(n5)
+    h2_m(n1)
+    h2_m(n2)
     h2_a(n2, n1)
-    w_forward(n4)
-    own_a(n0)
-    h2_a(n2, n2)
+    h2_a(n3, n1)
+    own_a_forward(n1)
+    w_issue(n6)
+    ag_a(n0)
+    ag_m(n0)
+    h2_m(n3)
+    h2_m(n4)
+    h2_m(n5)
     h2_a(n0, n2)
-    own_a_forward(n2)
+    h2_a(n3, n2)
+    h2_a(n3, n3)
+    ag_m(n1)
+    ag_a(n1)
     own_a_forward(n3)
-    own_a_forward(n1)
-    own_a_last(n3)
-    own_a_forward(n0)
-    w_forward(n5)
-    ag_a(n0)
-    h2_a(n1, n1)
-    h2_a(n3, n1)
-    h2_a(n3, n2)
+    h2_a(n0, n3)
+    w_ready(n5)
+    up(n2, n5, n6, n0, n4)
+    ag_m_forward(n0)
+    ag_m_forward(n1)
     h2_a(n1, n2)
-    w_issue(n6)
-    w_ready(n4)
-    up(n1, n4, n5, n0, n4)
-    own_a_last(n2)
-    ag_a(n1)
-    w_ready(n5)
-    up(n1, n5, n6, n0, n4)
-    ag_a(n2)
-    got(wo_hbm, sem("wout"))
+    ag_m(n2)
+    w_forward_near(n6)
     ag_a_forward(n0)
-    w_forward_near(n6)
     ag_a_forward(n1)
     up_near(n6)
-    ag_a_forward(n2)
     w_forward_far(n6)
+    h2_a(n2, n2)
+    own_a_last(n0)
+    ag_m_last(n0)
+    ag_m(n3)
+    own_a_last(n1)
+    ag_m_forward(n2)
+    h2_a(n2, n3)
+    ag_m(n4)
     up_far(n6)
     down_early_load()
     h1_b(n0)
+    late_start()
+    ag_m_last(n1)
     h1_b(n1)
+    h2_m(n6)
     h1_b(n2)
     h1_b(n3)
+    ag_m_forward(n3)
+    own_a_last(n3)
     h1_b(n4)
+    h2_b(n0)
+    h1_b(n5)
+    h1_b(n6)
+    h2_b(n1)
+    h2_b(n2)
+    ag_b(n0)
+    ag_b(n1)
+    h2_b(n3)
+    h2_b(n4)
+    own_a_last(n2)
     ag_a_last(n0)
-    h1_b(n5)
-    late_start()
+    h2_m(n7)
     ag_a_last(n1)
-    own_a_last(n0)
-    h2_b(n0)
-    own_a_last(n1)
+    ag_m_last(n2)
+    ag_b(n2)
+    ag_b_forward(n0)
+    h2_b(n5)
+    ag_b(n3)
+    h1_b(n7)
     down_early(n0, yes)
     down_early_load()
-    h2_a(n2, n3)
-    h2_a(n0, n3)
-    ag_b(n0)
-    h2_b(n1)
+    late_wait()
     h2_a(n1, n3)
-    h2_b(n2)
-    h2_b(n3)
-    h1_b(n6)
-    h1_b(n7)
+    ag_b_forward(n1)
+    ag_b_forward(n2)
+    ag_b(n4)
+    ag_a(n2)
+    ag_b_last(n0)
+    down_late(n0)
+    ag_m(n5)
+    y_send(n0)
+    h2_b(n6)
+    h2_b(n7)
     down_early(n1, yes)
     down_early_load()
-    h2_b(n4)
-    ag_b_forward(n0)
-    late_wait()
-    ag_b(n1)
-    h2_a(n3, n3)
-    h2_b(n5)
-    ag_b(n2)
-    h2_b(n6)
-    h2_b(n7)
-    ag_b_last(n0)
-    down_late(n0)
-    y_send(n0)
-    ag_b_forward(n1)
-    ag_b(n3)
+    ag_b_forward(n3)
+    ag_b_last(n2)
+    ag_b_last(n1)
+    ag_b_forward(n4)
+    y_forward(n0)
+    down_late(n1)
+    y_send(n1)
+    ag_m_last(n3)
+    ag_a_forward(n2)
+    down_late(n2)
+    y_final(n0)
+    ag_b(n5)
+    y_send(n2)
+    ag_m_forward(n4)
+    ag_m_forward(n5)
+    ag_b_last(n3)
+    ag_b_last(n4)
+    down_late(n3)
+    ag_a(n3)
     ag_a_last(n2)
+    y_send(n3)
+    y_forward(n1)
+    ag_b_forward(n5)
     down_early(n2, yes)
     down_early_load()
-    ag_b_forward(n2)
-    ag_b(n4)
-    y_forward(n0)
-    ag_b_last(n1)
-    ag_b(n5)
-    down_late(n1)
-    y_send(n1)
-    y_forward(n1)
-    ag_b_last(n2)
-    down_late(n2)
-    ag_b_forward(n3)
-    y_send(n2)
-    ag_b_forward(n4)
-    ag_b_forward(n5)
-    ag_a(n3)
+    ag_b(n6)
+    ag_m(n6)
+    y_forward(n3)
+    ag_m_last(n4)
+    down_late(n4)
+    ag_a_forward(n3)
+    ag_m_last(n5)
+    y_send(n4)
+    ag_m(n7)
+    ag_b_last(n5)
+    down_late(n5)
+    ag_b_forward(n6)
     y_forward(n2)
-    ag_b_last(n3)
-    down_late(n3)
-    y_send(n3)
-    ag_b_last(n4)
-    down_late(n4)
-    ag_b_last(n5)
-    y_send(n4)
-    y_final(n0)
-    ag_b(n6)
-    down_late(n5)
-    ag_a_forward(n3)
     y_send(n5)
-    ag_b_forward(n6)
     y_forward(n4)
     ag_b(n7)
+    ag_a_last(n3)
+    ag_m_forward(n6)
+    down_early(n3, yes)
+    ag_m_forward(n7)
+    y_final(n1)
     y_forward(n5)
-    y_forward(n3)
-    ag_a_last(n3)
-    down_early(n3, yes)
     ag_b_last(n6)
+    ag_b_forward(n7)
+    ag_m_last(n6)
     down_late(n6)
     y_send(n6)
-    ag_b_forward(n7)
-    y_final(n2)
-    y_final(n1)
-    y_forward(n6)
     ag_b_last(n7)
+    ag_m_last(n7)
     down_late(n7)
     y_send(n7)
+    y_final(n5)
+    y_final(n2)
+    y_forward(n6)
+    y_final(n4)
     y_final(n3)
-    y_final(n4)
+    y_forward(n7)
     y_final(n6)
-    y_forward(n7)
-    y_final(n5)
     y_final(n7)
     three = pl.ds(0, nx - 1)
     drain("stat", stat.at[three])
@@ -740,10 +802,11 @@
     drain("wout", wo_hbm)
     for kind in ("h1a", "h2a", "own"):
         drain(kind, hst_a.at[three])
-    for kind in ("h1b", "h2b"):
-        drain(kind, hst_b.at[three])
+    for part, hst, hf in (("m", hst_m, hf_m), ("b", hst_b, hf_b)):
+        drain("h1" + part, hst.at[three])
+        drain("h2" + part, hst.at[three])
+        drain("ag" + part, hf.at[:, :, :, three])
     drain("aga", hf_a.at[three, :, :, three])
-    drain("agb", hf_b.at[:, :, :, three])
     drain("y", acc.at[:, three])
 
 
@@ -756,8 +819,8 @@
         width = floc // nx
         tw = width // 7
         tiles = width // tw
-        early = tiles - LATE
-        ew, lw = early * tw, LATE * tw
+        early = tiles - MID - LATE
+        ew, mw, lw = early * tw, MID * tw, LATE * tw
         sub = tok // SUB
         piece = sub // ny
         bf, f32 = jnp.bfloat16, jnp.float32
@@ -771,6 +834,7 @@
                 hbm((tiles, 2 * nx, krows, tw), bf),
                 hbm(wout.shape, bf),
                 hbm((ny, SUB, nx, piece, ew), bf),
+                hbm((ny, SUB, nx, piece, mw), bf),
                 hbm((ny, SUB, nx, piece, lw), bf),
             ],
             in_specs=[
@@ -779,7 +843,7 @@
                 pl.BlockSpec(memory_space=pl.ANY),
                 pl.BlockSpec(memory_space=pl.ANY),
             ],
-            out_specs=[pl.BlockSpec(memory_space=pltpu.VMEM)] + [pl.BlockSpec(memory_space=pl.ANY)] * 4,
+            out_specs=[pl.BlockSpec(memory_space=pltpu.VMEM)] + [pl.BlockSpec(memory_space=pl.ANY)] * 5,
             scratch_shapes=[
                 pltpu.VMEM((tok, dloc), bf),
                 pltpu.VMEM((3, tok, 128), f32),
@@ -789,8 +853,10 @@
                 pltpu.VMEM((nx, ny, tok, dloc), bf),
                 pltpu.VMEM((3, ny, 2 * krows, tw), bf),
                 pltpu.VMEM((nx, ny, SUB, piece, ew), bf),
+                pltpu.VMEM((nx, ny, SUB, piece, mw), bf),
                 pltpu.VMEM((nx, ny, SUB, piece, lw), bf),
                 pltpu.VMEM((nx, SUB, nx, ny, piece, ew), bf),
+                pltpu.VMEM((nx, SUB, nx, ny, piece, mw), bf),
                 pltpu.VMEM((nx, SUB, nx, ny, piece, lw), bf),
                 pltpu.VMEM((SUB, nx, sub, dloc), f32),
                 pltpu.VMEM((nx, tok, tw), f32),

time: 327 us -> 324 us (level)
  Pallas kernels: 326 us -> 322 us
where the time goes in v5:
time: 324 us; the launch traced here: 323 us
  Pallas kernels  322 us (99%)
    pallas_call x1, Pallas kernels, local_block(): pl.pallas_call(functools.partial(block, (nx, ny, dloc * ny)), name='mlp_b...  322 us

profile of v5, /device:TPU:96, one launch (start us, length us, event | category | flops | bytes accessed | tf_op | source)
XLA Modules:
  0.0 323.5 jit_solution(1387777284341626371)
XLA Ops:
  0.0 322.5 %mlp_block.1 = (bf16[256,2048]{1,0:T(8,128)(2,1)S(1)}, bf16[7,8,1024,256]{3,2,1,0:T(8,128)(2,1)}, bf16[3584,2048]{1,0:T(8,128)(2,1)}, bf16[4,8,4,8,768]{4,3,2,1,...) custom-call(bf16[256,2048]{1,0:T(8,128)(2,1)} %x_hbm.1, f32[1,2048]{1,0:T(1,128)} %bitcast.1, ...), custom_call_target="tpu_custom_call" | custom-call | tf_op jit(solution)/shard_map/mlp_block/pallas_call | solution.py:829
  322.5 1.0 copy.6
